TPU v7x, 32 devices: a whole 2x2x4 slice. The times are simulated.
32 devices in a mesh: dp: 16 (over z, y, x), group: 2 (over core).
Axes of the slice: x: 2, y: 2, z: 4, core: 2. Of those that a mesh axis runs over, the one named last changes fastest.
Arguments:
- tokens: bfloat16 [25088, 512], P(('dp', 'group')), may hold values from -6 to 6
- cotangent: bfloat16 [25088, 512], P(('dp', 'group')), may hold values from -6 to 6
- counts: int32 [32], P(('dp', 'group')), may hold values from 2 to 16, as said below
- regions: int32 [25088], P(('dp', 'group')), may hold values from 0 to 8, as said below
- square_weights: float32 [4, 512, 512], P('group'), may hold values from -0.70710678 to 0.70710678
- wide_weights: float32 [2, 512, 2048], P('group'), may hold values from -0.25 to 0.25
- vectors: float32 [12, 512], replicated, may hold values from -1.2 to 1.4
- bias_table: float32 [169, 16], replicated, may hold values from -4 to 400
- square_moment: float32 [4, 512, 512], P('group'), may hold values from -64 to 64
- wide_moment: float32 [2, 512, 2048], P('group'), may hold values from -64 to 64
- vector_moment: float32 [12, 512], replicated, may hold values from -64 to 64
- table_moment: float32 [169, 16], replicated, may hold values from -7 to 7
Outputs:
- block_out: bfloat16 [25088, 512], P(('dp', 'group'))
- grad_tokens: bfloat16 [25088, 512], P(('dp', 'group'))
- grad_square: float32 [4, 512, 512], P('group')
- grad_wide: float32 [2, 512, 2048], P('group')
- grad_vectors: float32 [12, 512], replicated
- grad_table: float32 [169, 16], replicated
- new_square: float32 [4, 512, 512], P('group')
- new_wide: float32 [2, 512, 2048], P('group')
- new_vectors: float32 [12, 512], replicated
- new_table: float32 [169, 16], replicated
- new_square_moment: float32 [4, 512, 512], P('group')
- new_wide_moment: float32 [2, 512, 2048], P('group')
- new_vector_moment: float32 [12, 512], replicated
- new_table_moment: float32 [169, 16], replicated
Inputs may be any that keep to these rules, and one draw needn't show every extreme that they name: Entries 2 k and 2 k + 1 belong to the two devices of one group; their counts add to at most 20. Some device holds 16 windows beside a partner with 4. `regions`: each window's ids are one of the four layouts that a cyclic shift by 3 leaves in a 2 x 2 block of windows: all 0; 1 in local columns below 4 and 2 beyond; 3 in local rows below 4 and 6 beyond; 4, 5, 7, 8 by both.
All inputs are finite; a program needn't handle non-finite values.
Results may differ from a plain program's by a relative error of at most 0.012.
Values may be sent and summed in bfloat16 or wider, within the bound.
A program may use at most 128 MiB of HBM per device.

v0:
```python
import functools
import math

import jax
import jax.numpy as jnp
from jax import lax
from jax.experimental import pallas as pl
from jax.experimental.pallas import tpu as pltpu
from jax.sharding import PartitionSpec as P

HIGHEST = lax.Precision.HIGHEST
VECTOR_RATE = 0.05
TABLE_RATE = 1.0
D = 512
HEADS = 16
HEAD_DIM = 32
WIN = 7
WIN_DEV = 16
TOKW = 49
TABLE_ROWS = 169
MASKED = -1e30
EPSILON = 1e-05
MESH = pl.DeviceIdType.MESH

SLOTS_RUN = 10
TALL = 512
PADR = 528
TAIL0 = 480
TAIL = WIN_DEV * TOKW - TAIL0
JR = 56
IR = 64
GH = 8
GC = GH * HEAD_DIM
GL = GH * IR

f32, bf16 = jnp.float32, jnp.bfloat16


def exchange_kernel(sq_hbm, wide_hbm, tok_ref, cot_ref, meta_ref,
                    sq_out, wide_out, tok_out, cot_out, meta_out,
                    sq_in, wide_in, tok_land, sem_in, send, recv):
    dp, group = lax.axis_index("dp"), lax.axis_index("group")
    partner = (dp, 1 - group)
    ff = wide_hbm.shape[2]
    loads = [pltpu.make_async_copy(sq_hbm.at[m], sq_in.at[m], sem_in.at[m]) for m in range(2)]
    loads += [pltpu.make_async_copy(wide_hbm.at[0, pl.ds(128 * c, 128)], wide_in.at[pl.ds(128 * c, 128)], sem_in.at[2 + c])
              for c in range(4)]
    for c in loads:
        c.start()
    barrier = pltpu.get_barrier_semaphore()
    pl.semaphore_signal(barrier, inc=1, device_id=partner, device_id_type=MESH)
    pl.semaphore_wait(barrier, 1)

    def remote(src, dst, k):
        return pltpu.make_async_remote_copy(src_ref=src, dst_ref=dst, send_sem=send.at[k], recv_sem=recv.at[k],
                                            device_id=partner, device_id_type=MESH)

    copies = [remote(meta_ref, meta_out, 6),
              remote(tok_ref.at[pl.ds(TAIL0, TAIL)], tok_out, 7),
              remote(cot_ref.at[pl.ds(TAIL0, TAIL)], cot_out, 8)]
    for c in copies:
        c.start()
    for m in range(2):
        loads[m].wait()

        def body(k, carry):
            r = pl.multiple_of(k * 32, 32)
            sq_out[group, m, pl.ds(r, 32)] = sq_in[m, pl.ds(r, 32)].astype(bf16)
            return carry
        lax.fori_loop(0, D // 32, body, 0)
        c = remote(sq_out.at[group, m], sq_out.at[group, m], m)
        c.start()
        copies.append(c)
    for q in range(4):
        loads[2 + q].wait()

        def body(k, carry):
            r = pl.multiple_of(q * 128 + k * 16, 16)
            wide_out[group, pl.ds(r, 16)] = wide_in[pl.ds(r, 16)].astype(bf16)
            return carry
        lax.fori_loop(0, 8, body, 0)
        piece = pl.ds(128 * q, 128)
        c = remote(wide_out.at[group, piece], wide_out.at[group, piece], 2 + q)
        c.start()
        copies.append(c)
    for c in copies:
        c.wait()


def exchange(sq, wide, tok, cot, meta):
    vmem, any_ = pl.BlockSpec(memory_space=pltpu.VMEM), pl.BlockSpec(memory_space=pl.ANY)
    ff = wide.shape[2]
    return pl.pallas_call(
        exchange_kernel,
        out_shape=(
            jax.ShapeDtypeStruct((2, 2, D, D), bf16),
            jax.ShapeDtypeStruct((2, D, ff), bf16),
            jax.ShapeDtypeStruct((TAIL, D), bf16),
            jax.ShapeDtypeStruct((TAIL, D), bf16),
            jax.ShapeDtypeStruct(meta.shape, jnp.int32),
        ),
        in_specs=[any_, any_, vmem, vmem, vmem],
        out_specs=(vmem,) * 5,
        scratch_shapes=[pltpu.VMEM((2, D, D), f32), pltpu.VMEM((D, ff), f32), pltpu.VMEM((8, 128), f32),
                        pltpu.SemaphoreType.DMA((6,)), pltpu.SemaphoreType.DMA((9,)), pltpu.SemaphoreType.DMA((9,))],
        compiler_params=pltpu.CompilerParams(collective_id=0, has_side_effects=True, vmem_limit_bytes=32 * 2**20),
        name="exchange_weights",
    )(sq, wide, tok, cot, meta)


def nt(a, b):
    return lax.dot_general(a, b, (((1,), (1,)), ((), ())), preferred_element_type=f32)


def tn(a, b):
    return lax.dot_general(a, b, (((0,), (0,)), ((), ())), preferred_element_type=f32)


def nn(a, b):
    return jnp.dot(a, b, preferred_element_type=f32)


def loop_rows(fn, total=TALL, step=64):
    def body(k, carry):
        fn(pl.ds(pl.multiple_of(k * step, step), step))
        return carry
    lax.fori_loop(0, total // step, body, 0)


def block_kernel(mine, theirs, tok, cot, tok_tail, cot_tail, sq, wide, vec, bias,
                 out, out_tail, gtok, gtok_tail, grads, gvec, gtab,
                 x, e, norm, inv, h1, hT, qkv, mask_bias, probs, o, h2, eb, act, dact, u_s, y, dh, dx, dO, wins, dwin, tail_f):
    count = jnp.minimum(mine[0, 0], SLOTS_RUN)
    extra = jnp.maximum(theirs[0, 0] - SLOTS_RUN, 0)
    ff = wide.shape[2]
    chunks = ff // D
    scale = HEAD_DIM ** (-0.5)

    def fill(src, src_tail, dst, masked):
        def body(rows, own):
            v = own.astype(f32)
            if masked:
                index = rows.start + lax.broadcasted_iota(jnp.int32, (rows.size, 1), 0)
                v = jnp.where(index < count * TOKW, v, 0.0)
            dst[rows] = v
        loop_rows(lambda rows: body(rows, src[rows]), 512, 64)
        dst[pl.ds(SLOTS_RUN * TOKW, PADR - SLOTS_RUN * TOKW)] = jnp.zeros((PADR - SLOTS_RUN * TOKW, D), f32)
        loop_rows(lambda rows: tail_f.__setitem__(rows, src_tail[rows].astype(f32)), TAIL, 16)

        for k in range(WIN_DEV - SLOTS_RUN):
            @pl.when(k < extra)
            def _():
                dst[pl.ds((SLOTS_RUN - 1 - k) * TOKW, TOKW)] = tail_f[pl.ds(SLOTS_RUN * TOKW - TAIL0 + k * TOKW, TOKW)]

    fill(tok, tok_tail, x, False)
    fill(cot, cot_tail, e, True)

    def bias_body(c, carry):
        cs = pl.ds(pl.multiple_of(c * 128, 128), 128)
        j = lax.broadcasted_iota(jnp.int32, (JR, 128), 0)
        i = lax.broadcasted_iota(jnp.int32, (JR, 128), 1) & (IR - 1)
        aj, ai = (j * 37) >> 8, (i * 37) >> 8
        bj, bi = j - 7 * aj, i - 7 * ai
        inside = j < TOKW
        same_row = (aj >= 4) == (ai >= 4)
        same_col = (bj >= 4) == (bi >= 4)
        pad = i >= TOKW
        base = bias[:, cs]
        mask_bias[0, :, cs] = jnp.where(inside, base, MASKED)
        mask_bias[1, :, cs] = jnp.where(inside & (same_col | pad), base, MASKED)
        mask_bias[2, :, cs] = jnp.where(inside & (same_row | pad), base, MASKED)
        mask_bias[3, :, cs] = jnp.where(inside & ((same_row & same_col) | pad), base, MASKED)
        return carry
    lax.fori_loop(0, HEADS * IR // 128, bias_body, 0)

    def norm_rows(src, gain, shift, low, k):
        def body(rows):
            v = src[rows]
            center = v - jnp.mean(v, axis=1, keepdims=True)
            r = lax.rsqrt(jnp.mean(center * center, axis=1, keepdims=True) + EPSILON)
            n = center * r
            norm[k, rows] = n
            inv[k, rows] = jnp.broadcast_to(r, (rows.size, 128))
            low[rows] = (n * gain + shift).astype(bf16)
        loop_rows(body)

    norm_rows(x, vec[0:1], vec[2:3], h1, 0)

    def project(m, carry):
        shift = jnp.where(m == 0, vec[4:5], jnp.where(m == 2, vec[5:6], jnp.zeros((1, D), f32)))
        qkv[m, pl.ds(0, TALL)] = nn(h1[...], sq[m]) + shift
        return carry
    lax.fori_loop(0, 3, project, 0)
    o[pl.ds(TALL - 24, PADR - TALL + 24)] = jnp.zeros((PADR - TALL + 24, D), f32)
    live_i = lax.broadcasted_iota(jnp.int32, (IR, 1), 0) < TOKW

    def spread_windows(src, dst):
        for w in range(SLOTS_RUN):
            def body(c, carry):
                cs = pl.ds(pl.multiple_of(c * 128, 128), 128)
                dst[pl.ds(w * IR, IR), cs] = jnp.where(live_i, src[pl.ds(w * TOKW, IR), cs], 0.0).astype(bf16)
                return carry
            lax.fori_loop(0, D // 128, body, 0)

    def pack_windows(src, dst):
        for w in range(SLOTS_RUN):
            def body(c, carry):
                cs = pl.ds(pl.multiple_of(c * 128, 128), 128)
                dst[pl.ds(w * TOKW, TOKW), cs] = src[pl.ds(w * IR, TOKW), cs]
                return carry
            lax.fori_loop(0, D // 128, body, 0)

    for m in range(3):
        spread_windows(qkv.at[m], wins.at[m])

    lane_head = lax.broadcasted_iota(jnp.int32, (GH, 1, GC), 2) >> 5
    row_head = lax.broadcasted_iota(jnp.int32, (GH, 1, GC), 0)
    pick = lane_head == row_head
    pick_f = pick.astype(f32)
    pick_b = pick_f.astype(bf16)

    def spread(b):
        return (b[None] * pick_b).reshape(GL, GC)

    def gather(result):
        return jnp.sum(result.reshape(GH, IR, GC) * pick_f, axis=0)

    def place(t):
        w, hg = lax.div(t, 2), lax.rem(t, 2)
        return w, pl.multiple_of(w * IR, IR), pl.ds(pl.multiple_of(hg * GC, 128), GC), pl.ds(pl.multiple_of(hg * GL, 128), GL)

    def kind_of(w):
        own = mine[0, 1 + w]
        other = theirs[0, 1 + jnp.maximum(2 * SLOTS_RUN - 1 - w, SLOTS_RUN) % WIN_DEV]
        region = jnp.where(w >= SLOTS_RUN - extra, other, own)
        return jnp.where(region == 1, 1, jnp.where(region == 3, 2, jnp.where(region == 4, 3, 0)))

    def attend(t, carry):
        w, row, cs, ls = place(t)
        qd = spread(wins[0, pl.ds(row, IR), cs])
        kb = wins[1, pl.ds(row, JR), cs]
        vb = wins[2, pl.ds(row, JR), cs]
        s = nt(kb, qd) * scale + mask_bias[kind_of(w), :, ls]
        top = jnp.max(s, axis=0, keepdims=True)
        p = jnp.exp(s - top)
        p = p * (1.0 / jnp.sum(p, axis=0, keepdims=True))
        probs[t] = p
        dwin[0, pl.ds(row, IR), cs] = gather(tn(p.astype(bf16), vb))
        return carry
    lax.fori_loop(0, 2 * SLOTS_RUN, attend, 0)

    pack_windows(dwin.at[0], o)

    ob = h2
    loop_rows(lambda rows: ob.__setitem__(rows, o[rows].astype(bf16)))
    y[...] = x[pl.ds(0, TALL)] + (nn(ob[...], sq[3]) + vec[6:7])
    hT[0] = o[pl.ds(0, TALL)].T.astype(bf16)
    norm_rows(y, vec[1:2], vec[3:4], h2, 1)
    hT[1] = h2[...].astype(f32).T.astype(bf16)
    hT[2] = e[pl.ds(0, TALL)].T.astype(bf16)
    loop_rows(lambda rows: eb.__setitem__(rows, e[rows].astype(bf16)))
    dh[...] = jnp.zeros((TALL, D), f32)

    def feed(c, carry):
        cs = pl.ds(pl.multiple_of(c * D, 128), D)
        u_s[...] = nn(h2[...], wide[0, :, cs]) + vec[pl.ds(8 + c, 1)]
        dh_c = nn(eb[...], wide[1, :, cs])
        dO[pl.ds(0, TALL)] = dh_c

        def body(rows):
            u = u_s[rows]
            cdf = 0.5 * (1.0 + lax.erf(u * 0.7071067811865476))
            density = jnp.exp(-0.5 * u * u) * 0.3989422804014327
            act[rows] = (u * cdf).astype(bf16)
            dact[rows] = (dO[rows] * (cdf + u * density)).astype(bf16)
        loop_rows(body, TALL, 16)
        y[...] += nt(act[...], wide[1, :, cs])
        dh[...] += nt(dact[...], wide[0, :, cs])
        grads[1, 2 + c] = nn(hT[2], act[...]).astype(bf16)
        grads[0, 2 + c] = nn(hT[1], dact[...]).astype(bf16)
        gvec[pl.ds(8 + c, 1)] = jnp.sum(dact[...].astype(f32), axis=0, keepdims=True)
        return carry
    lax.fori_loop(0, chunks, feed, 0)

    def norm_back(grad, gain, k, add, dst):
        zero = jnp.zeros((1, D), f32)

        def body(i, carry):
            rows = pl.ds(pl.multiple_of(i * 64, 64), 64)
            g_gain, g_shift = carry
            g = grad[rows]
            n = norm[k, rows]
            dn = g * gain
            r = inv[k, rows][:, :1]
            dst[rows] = add[rows] + r * (dn - jnp.mean(dn, axis=1, keepdims=True)
                                         - n * jnp.mean(dn * n, axis=1, keepdims=True))
            return (g_gain + jnp.sum(g * n, axis=0, keepdims=True), g_shift + jnp.sum(g, axis=0, keepdims=True))
        return lax.fori_loop(0, TALL // 64, body, (zero, zero))

    gvec[1:2], gvec[3:4] = norm_back(dh, vec[1:2], 1, e, dx)
    gvec[7:8] = jnp.sum(e[pl.ds(0, TALL)], axis=0, keepdims=True)

    def put(src, dst, dst_tail):
        def own(rows):
            index = rows.start + lax.broadcasted_iota(jnp.int32, (rows.size, 1), 0)
            dst[rows] = jnp.where(index < count * TOKW, src[rows], 0.0).astype(bf16)
        loop_rows(own, 512, 64)
        dst[pl.ds(512, WIN_DEV * TOKW - 512)] = jnp.zeros((WIN_DEV * TOKW - 512, D), bf16)
        tail_f[...] = jnp.zeros((TAIL + 16, D), f32)

        for k in range(WIN_DEV - SLOTS_RUN):
            @pl.when(k < extra)
            def _():
                tail_f[pl.ds(SLOTS_RUN * TOKW - TAIL0 + k * TOKW, TOKW)] = src[pl.ds((SLOTS_RUN - 1 - k) * TOKW, TOKW)]
        loop_rows(lambda rows: dst_tail.__setitem__(rows, tail_f[rows].astype(bf16)), TAIL, 16)

    y[...] += vec[7:8]
    put(y, out, out_tail)

    loop_rows(lambda rows: eb.__setitem__(rows, dx[rows].astype(bf16)))
    gvec[6:7] = jnp.sum(eb[...].astype(f32), axis=0, keepdims=True)
    grads[1, 1] = nn(hT[0], eb[...]).astype(bf16)
    dO[pl.ds(0, TALL)] = nt(eb[...], sq[3])
    spread_windows(dO, wins.at[3])
    gtab[...] = jnp.zeros((JR, HEADS * IR), f32)

    def attend_back(t, carry):
        w, row, cs, ls = place(t)
        dd = spread(wins[3, pl.ds(row, IR), cs])
        qd = spread(wins[0, pl.ds(row, IR), cs])
        kb = wins[1, pl.ds(row, JR), cs]
        vb = wins[2, pl.ds(row, JR), cs]
        p = probs[t]
        dp = nt(vb, dd)
        dwin[2, pl.ds(row, JR), cs] = nn(p.astype(bf16), dd)
        ds = p * (dp - jnp.sum(p * dp, axis=0, keepdims=True))
        dsb = ds.astype(bf16)
        gtab[:, ls] += dsb.astype(f32)
        dwin[1, pl.ds(row, JR), cs] = nn(dsb, qd) * scale
        dwin[0, pl.ds(row, IR), cs] = gather(tn(dsb, kb)) * scale
        return carry
    lax.fori_loop(0, 2 * SLOTS_RUN, attend_back, 0)

    for m in range(3):
        qkv[m, pl.ds(TALL - 24, PADR - TALL + 24)] = jnp.zeros((PADR - TALL + 24, D), f32)
        pack_windows(dwin.at[m], qkv.at[m])
    hT[0] = h1[...].astype(f32).T.astype(bf16)
    dh[...] = jnp.zeros((TALL, D), f32)

    def input_grads(m, carry):
        loop_rows(lambda rows: eb.__setitem__(rows, qkv[m, rows].astype(bf16)))
        total = jnp.sum(eb[...].astype(f32), axis=0, keepdims=True)

        @pl.when(m == 0)
        def _():
            gvec[4:5] = total

        @pl.when(m == 2)
        def _():
            gvec[5:6] = total
        dh[...] += nt(eb[...], sq[m])
        grads[lax.div(m, 2), lax.rem(m, 2)] = nn(hT[0], eb[...]).astype(bf16)
        return carry
    lax.fori_loop(0, 3, input_grads, 0)
    gvec[0:1], gvec[2:3] = norm_back(dh, vec[0:1], 0, dx, y)
    put(y, gtok, gtok_tail)


def block(mine, theirs, tok, cot, tok_tail, cot_tail, sq, wide, vec, bias):
    vmem, smem = pl.BlockSpec(memory_space=pltpu.VMEM), pl.BlockSpec(memory_space=pltpu.SMEM)
    ff = wide.shape[2]
    V = pltpu.VMEM
    return pl.pallas_call(
        block_kernel,
        out_shape=(
            jax.ShapeDtypeStruct(tok.shape, bf16), jax.ShapeDtypeStruct((TAIL, D), bf16),
            jax.ShapeDtypeStruct(tok.shape, bf16), jax.ShapeDtypeStruct((TAIL, D), bf16),
            jax.ShapeDtypeStruct((2, 2 + ff // D, D, D), bf16),
            jax.ShapeDtypeStruct(vec.shape, f32),
            jax.ShapeDtypeStruct((JR, HEADS * IR), f32),
        ),
        in_specs=[smem, smem] + [vmem] * 8,
        out_specs=(vmem,) * 7,
        scratch_shapes=[
            V((PADR, D), f32), V((PADR, D), f32), V((2, TALL, D), f32), V((2, TALL, 128), f32),
            V((TALL, D), bf16), V((3, D, TALL), bf16), V((3, PADR, D), f32), V((4, JR, HEADS * IR), f32),
            V((2 * SLOTS_RUN, JR, GL), f32), V((PADR, D), f32), V((TALL, D), bf16), V((TALL, D), bf16),
            V((TALL, D), bf16), V((TALL, D), bf16), V((TALL, D), f32), V((TALL, D), f32), V((TALL, D), f32),
            V((TALL, D), f32), V((PADR, D), f32), V((4, SLOTS_RUN * IR, D), bf16), V((3, SLOTS_RUN * IR, D), f32), V((TAIL + 16, D), f32),
        ],
        compiler_params=pltpu.CompilerParams(vmem_limit_bytes=58 * 2**20),
        name="window_block",
    )(mine, theirs, tok, cot, tok_tail, cot_tail, sq.reshape(4, D, D), wide, vec, bias)


def relative_onehot_t():
    j = jnp.arange(TOKW)[:, None]
    i = jnp.arange(IR)[None, :]
    rel = (i // WIN - j // WIN + WIN - 1) * (2 * WIN - 1) + i % WIN - j % WIN + WIN - 1
    hot = (rel[:, :, None] == jnp.arange(TABLE_ROWS)) & (i < TOKW)[:, :, None]
    return hot.astype(f32)


BLK = 512
HALF = 6
ORDER = (2, 3, 4, 5, 0, 1)
SMALL = 40


def chip_grid(dp):
    side = max(1, math.isqrt(dp // 4))
    if side * side * 4 == dp:
        return (side, side, 4)
    return (1, 1, dp)


class Lane:
    def __init__(self, size, pos, stride, dp, group):
        self.n, self.i, self.stride, self.dp, self.group = size, pos, stride, dp, group

    def peer(self, delta):
        return (self.dp + delta * self.stride, self.group)


class Ids:
    def __init__(self):
        self.count = 0

    def take(self, number=1):
        first = self.count
        self.count += number
        return first


def lanes(sizes):
    dp, group = lax.axis_index("dp"), lax.axis_index("group")
    nx, ny, nz = sizes
    x, y, z = lax.rem(dp, nx), lax.rem(lax.div(dp, nx), ny), lax.div(dp, nx * ny)
    return (
        Lane(nx, x, 1, dp, group),
        Lane(ny, y, nx, dp, group),
        Lane(nz, z, nx * ny, dp, group),
    )


class Plan:
    def __init__(self, sizes, pieces):
        nx, ny, nz = sizes
        self.orders = ((0, 2, 1), (1, 2, 0))
        self.rs, self.ag = Ids(), Ids()
        self.rows = 0
        self.slots = {}
        half = BLK // 2
        for piece in range(pieces):
            color = piece % 2
            rows = half
            for stage, dim in enumerate(self.orders[color]):
                n = sizes[dim]
                if stage < 2:
                    rows = rows // n
                land = {}
                for way in ("R", "L"):
                    for j in range(n):
                        if (way == "R" and j > 0) or (way == "L" and j < n - 1):
                            land[way, j] = (self.rs.take(), self.rows)
                            self.rows += rows
                ag_recv = self.ag.take(n)
                self.slots[piece, stage] = (land, ag_recv)


def make_comm(sizes):
    pieces = 2 * HALF
    plan = Plan(sizes, pieces)

    def tasks_for(piece, env):
        (lane_all, own_ref, core_land, acc, out_ref, land_ref, rs_send, rs_recv, ag_sl, ag_sr, ag_recv,
         core_send_sem, core_recv_sem, partner, ends, grads_ref) = env
        color = piece % 2
        block = ORDER[piece // 2]
        base = color * (BLK // 2)
        half = BLK // 2
        order = plan.orders[color]
        dims = [lane_all[d] for d in order]
        tasks = []

        def add_into(dst, dst_rows, dst_cols, src_row, rows, cols_w, col0=0):
            step = min(rows, 32)

            def body(k, carry):
                r = pl.multiple_of(dst_rows + k * step, 16)
                s = pl.multiple_of(src_row + k * step, 16)
                here = acc[block, pl.ds(r, step), dst_cols].astype(jnp.float32)
                there = land_ref[pl.ds(s, step), pl.ds(0, cols_w)].astype(jnp.float32)
                dst[block, pl.ds(r, step), dst_cols] = (here + there).astype(jnp.bfloat16)
                return carry

            if rows == step:
                body(0, 0)
            else:
                lax.fori_loop(0, rows // step, body, 0)

        all_cols = pl.ds(0, BLK)

        r_sizes = [half // dims[0].n, half // dims[0].n // dims[1].n]
        off0 = base
        off1 = off0 + dims[0].i * r_sizes[0]
        off2 = off1 + dims[1].i * r_sizes[1]
        cols = BLK // dims[2].n

        def view(stage, j):
            if stage == 0:
                return pl.multiple_of(off0 + j * r_sizes[0], 16), r_sizes[0], pl.ds(0, BLK), BLK
            if stage == 1:
                return pl.multiple_of(off1 + j * r_sizes[1], 16), r_sizes[1], pl.ds(0, BLK), BLK
            start = j * cols if isinstance(j, int) else pl.multiple_of(j * cols, 128)
            return pl.multiple_of(off2, 16), r_sizes[1], pl.ds(start, cols), cols

        def rs_copy(stage, way, j):
            land, _ = plan.slots[piece, stage]
            sem, row = land[way, j]
            lane = dims[stage]
            r, rows, cs, width = view(stage, j)
            return pltpu.make_async_remote_copy(
                src_ref=acc.at[block, pl.ds(r, rows), cs],
                dst_ref=land_ref.at[pl.ds(row, rows), pl.ds(0, width)],
                send_sem=rs_send.at[sem],
                recv_sem=rs_recv.at[sem],
                device_id=lane.peer(1 if way == "R" else -1),
                device_id_type=MESH,
            )

        def rs_tick(stage, h):
            lane = dims[stage]
            n = lane.n
            land, _ = plan.slots[piece, stage]
            last = stage == 2

            @pl.when(lane.i == h)
            def _():
                for j in range(n - 1, h - 1, -1):
                    if h > 0:
                        rs_copy(stage, "R", j).wait_recv()
                        r, rows, cs, width = view(stage, j)
                        add_into(acc, r, cs, land["R", j][1], rows, width)
                    if j > h:
                        rs_copy(stage, "R", j).start()

            @pl.when(lane.i == n - 1 - h)
            def _():
                for j in range(0, n - h):
                    if h > 0:
                        rs_copy(stage, "L", j).wait_recv()
                        r, rows, cs, width = view(stage, j)
                        add_into(acc, r, cs, land["L", j][1], rows, width)
                    if j < n - 1 - h:
                        rs_copy(stage, "L", j).start()

        def rs_end(stage):
            lane = dims[stage]
            n = lane.n
            for j in range(n):
                if j > 0:
                    @pl.when(lane.i < j)
                    def _():
                        rs_copy(stage, "R", j).wait_send()
                if j < n - 1:
                    @pl.when(lane.i > j)
                    def _():
                        rs_copy(stage, "L", j).wait_send()

        def ag_copy(stage, j, way):
            _, first = plan.slots[piece, stage]
            lane = dims[stage]
            r, rows, cs, width = view(stage, j)
            piece_ref = out_ref.at[block, pl.ds(r, rows), cs]
            return pltpu.make_async_remote_copy(
                src_ref=piece_ref,
                dst_ref=piece_ref,
                send_sem=(ag_sr if way > 0 else ag_sl).at[first + j],
                recv_sem=ag_recv.at[first + j],
                device_id=lane.peer(way),
                device_id_type=MESH,
            )

        def ag_tick(stage, h):
            lane = dims[stage]
            n, i = lane.n, lane.i
            if h == 0:
                @pl.when(i < n - 1)
                def _():
                    ag_copy(stage, i, 1).start()

                @pl.when(i > 0)
                def _():
                    ag_copy(stage, i, -1).start()
                return

            @pl.when(i >= h)
            def _():
                ag_copy(stage, i - h, -1).wait_recv()

                @pl.when(i < n - 1)
                def _():
                    ag_copy(stage, i - h, 1).start()

            @pl.when(i + h <= n - 1)
            def _():
                ag_copy(stage, i + h, 1).wait_recv()

                @pl.when(i > 0)
                def _():
                    ag_copy(stage, i + h, -1).start()

        def ag_end(stage):
            lane = dims[stage]
            n, i = lane.n, lane.i
            for h in range(n):
                @pl.when((i >= h) & (i < n - 1))
                def _():
                    ag_copy(stage, i - h, 1).wait_send()

                @pl.when((i + h <= n - 1) & (i > 0))
                def _():
                    ag_copy(stage, i + h, -1).wait_send()

        def core_copy():
            return pltpu.make_async_remote_copy(
                src_ref=grads_ref.at[1 - partner[2], block, pl.ds(base, half)],
                dst_ref=core_land.at[block, pl.ds(base, half)],
                send_sem=core_send_sem.at[piece],
                recv_sem=core_recv_sem.at[piece],
                device_id=partner[:2],
                device_id_type=MESH,
            )

        def first():
            core_copy().wait_recv()

            def body(k, carry):
                r = pl.multiple_of(base + k * 32, 16)
                here = grads_ref[partner[2], block, pl.ds(r, 32)].astype(jnp.float32)
                there = core_land[block, pl.ds(r, 32)].astype(jnp.float32)
                acc[block, pl.ds(r, 32)] = (here + there).astype(jnp.bfloat16)
                return carry

            lax.fori_loop(0, half // 32, body, 0)

        def copy_out():
            r, rows, cs, width = view(2, dims[2].i)
            out_ref[block, pl.ds(r, rows), cs] = acc[block, pl.ds(r, rows), cs]

        flat = [first]
        groups = []
        for stage in range(3):
            for h in range(dims[stage].n):
                groups.append((h == 0, functools.partial(rs_tick, stage, h)))
        groups.append((False, copy_out))
        for stage in (2, 1, 0):
            for h in range(dims[stage].n):
                groups.append((h == 0, functools.partial(ag_tick, stage, h)))
        ticks = [[first]]
        for joined, task in groups:
            if joined or task is copy_out:
                ticks[-1].append(task)
            else:
                ticks.append([task])
        for stage in range(3):
            ends.append(functools.partial(rs_end, stage))
            ends.append(functools.partial(ag_end, stage))
        ends.append(lambda: core_copy().wait_send())
        return core_copy, ticks

    def kernel(grads_ref, small_ref, tail_a, tail_b, out_ref, small_out, back_a, back_b, core_land, acc, land_ref, small_core, small_land,
               rs_send, rs_recv, ag_sl, ag_sr, ag_recv, core_s, core_r, sm_cs, sm_cr, sm_s, sm_r, bk_s, bk_r, *, delta):
        lane_all = lanes(sizes)
        dp, group = lax.axis_index("dp"), lax.axis_index("group")
        partner = (dp, 1 - group, group)

        barrier = pltpu.get_barrier_semaphore()
        total = 1
        pl.semaphore_signal(barrier, inc=1, device_id=partner[:2], device_id_type=MESH)
        for lane in lane_all:
            for k in range(1, lane.n):
                to = lax.rem(lane.i + k, lane.n)
                pl.semaphore_signal(barrier, inc=1, device_id=lane.peer(to - lane.i), device_id_type=MESH)
                total += 1
        pl.semaphore_wait(barrier, total)

        ends = []
        env = (lane_all, None, core_land, acc, out_ref, land_ref, rs_send, rs_recv, ag_sl, ag_sr, ag_recv,
               core_s, core_r, partner, ends, grads_ref)

        def sm_core():
            return pltpu.make_async_remote_copy(
                src_ref=small_ref.at[1 - group], dst_ref=small_core, send_sem=sm_cs.at[0], recv_sem=sm_cr.at[0],
                device_id=partner[:2], device_id_type=MESH)

        def sm_back():
            return pltpu.make_async_remote_copy(
                src_ref=small_out.at[group], dst_ref=small_out.at[group], send_sem=sm_cs.at[1], recv_sem=sm_cr.at[1],
                device_id=partner[:2], device_id_type=MESH)

        first_slot = [0, sizes[0], sizes[0] + sizes[1]]

        def sm_copy(d, k):
            lane = lane_all[d]
            to = lax.rem(lane.i + k, lane.n)
            return pltpu.make_async_remote_copy(
                src_ref=small_land.at[first_slot[d] + lane.i],
                dst_ref=small_land.at[first_slot[d] + lane.i],
                send_sem=sm_s.at[first_slot[d] + k],
                recv_sem=sm_r.at[first_slot[d] + lane.i],
                device_id=lane.peer(to - lane.i), device_id_type=MESH)

        def sm_wait(d, k):
            lane = lane_all[d]
            source = lax.rem(lane.i + k, lane.n)
            pltpu.make_async_remote_copy(
                src_ref=small_land.at[first_slot[d] + source],
                dst_ref=small_land.at[first_slot[d] + source],
                send_sem=sm_s.at[first_slot[d] + k],
                recv_sem=sm_r.at[first_slot[d] + source],
                device_id=lane.peer(source - lane.i), device_id_type=MESH).wait_recv()

        def sm_start(d, value):
            lane = lane_all[d]
            small_land[first_slot[d] + lane.i] = value
            for k in range(1, lane.n):
                sm_copy(d, k).start()

        def sm_finish(d):
            lane = lane_all[d]
            for k in range(1, lane.n):
                sm_wait(d, k)
            value = small_land[first_slot[d]]
            for j in range(1, lane.n):
                value = value + small_land[first_slot[d] + j]
            return value

        def sm0():
            sm_core().wait_recv()
            sm_start(0, small_ref[group] + small_core[...])

        def sm1():
            sm_start(1, sm_finish(0))

        def sm2():
            sm_start(2, sm_finish(1))

        def sm3():
            small_out[group] = sm_finish(2)
            sm_back().start()

        def sm4():
            sm_back().wait_recv()

        def back(k):
            return pltpu.make_async_remote_copy(
                src_ref=(tail_a, tail_b)[k], dst_ref=(back_a, back_b)[k], send_sem=bk_s.at[k], recv_sem=bk_r.at[k],
                device_id=partner[:2], device_id_type=MESH)

        sm_core().start()
        made = [tasks_for(p, env) for p in range(pieces)]
        for core_copy, _ in made:
            core_copy().start()
        for k in range(2):
            back(k).start()
        table = {}
        length = max(len(t) for _, t in made)
        for p, (_, ticks) in enumerate(made):
            for k, tick in enumerate(ticks):
                table.setdefault(int(delta * (p // 2)) + k, []).append((p, tick))
        for k, task in enumerate((sm0, sm1, sm2, sm3, sm4)):
            table.setdefault(1 + 2 * k, []).append((-1, [task]))
        for when in sorted(table):
            for p, tick in sorted(table[when], key=lambda e: e[0]):
                for task in tick:
                    task()
        for task in ends:
            task()
        for k in range(2):
            back(k).wait()
        sm_core().wait_send()
        sm_back().wait_send()
        for d in range(3):
            for k in range(1, sizes[d]):
                sm_copy(d, k).wait_send()

    def call(grads, small, tail_a, tail_b, delta=1.0):
        dma = pltpu.SemaphoreType.DMA
        vmem = pl.BlockSpec(memory_space=pltpu.VMEM)
        return pl.pallas_call(
            functools.partial(kernel, delta=delta),
            out_shape=(
                jax.ShapeDtypeStruct((HALF, BLK, BLK), jnp.bfloat16),
                jax.ShapeDtypeStruct((2, SMALL, 128), jnp.float32),
                jax.ShapeDtypeStruct(tail_a.shape, tail_a.dtype),
                jax.ShapeDtypeStruct(tail_b.shape, tail_b.dtype),
            ),
            in_specs=[vmem, vmem, vmem, vmem],
            out_specs=[vmem, vmem, vmem, vmem],
            scratch_shapes=[
                pltpu.VMEM((HALF, BLK, BLK), jnp.bfloat16),
                pltpu.VMEM((HALF, BLK, BLK), jnp.bfloat16),
                pltpu.VMEM((plan.rows, BLK), jnp.bfloat16),
                pltpu.VMEM((SMALL, 128), jnp.float32),
                pltpu.VMEM((sum(sizes), SMALL, 128), jnp.float32),
                dma((plan.rs.count,)),
                dma((plan.rs.count,)),
                dma((plan.ag.count,)),
                dma((plan.ag.count,)),
                dma((plan.ag.count,)),
                dma((pieces,)),
                dma((pieces,)),
                dma((2,)),
                dma((2,)),
                dma((sum(sizes),)),
                dma((sum(sizes),)),
                dma((2,)),
                dma((2,)),
            ],
            compiler_params=pltpu.CompilerParams(
                collective_id=1, has_side_effects=True, vmem_limit_bytes=56 * 2**20
            ),
            name="reduce_gradients",
        )(grads, small, tail_a, tail_b)

    return call


MOMENTUM = 0.9
MATRIX_RATE = 0.4
NEWTON_ONE = 3.4445
NEWTON_TWO = -4.775
NEWTON_THREE = 2.0315
STEP = 32


def muon_kernel(g_hbm, sw_hbm, ww_hbm, sm_hbm, wm_hbm, row_a, row_b, back_a, back_b,
                gs_out, gw_out, ns_out, nw_out, nsm_out, nwm_out, out_a, out_b,
                g, sw, ww, sm, wm, gs, gw, xs, xw, gram, mix, own, back, sem_in, sem_out, sem_row):
    ff = ww.shape[2]
    cols = ff // D

    def load(src, dst, k):
        return pltpu.make_async_copy(src, dst, sem_in.at[k])

    loads = [load(g_hbm.at[pl.ds(0, 2)], g.at[pl.ds(0, 2)], 0), load(sm_hbm, sm, 1),
             load(g_hbm.at[pl.ds(2, cols)], g.at[pl.ds(2, cols)], 2), load(wm_hbm, wm, 3),
             load(sw_hbm, sw, 4), load(ww_hbm, ww, 5)]
    for c in loads:
        c.start()
    first, rows = row_a.shape[0] - back.shape[1], back.shape[1]
    fetch, put = [], []
    for k, (mine, theirs, out) in enumerate(((row_a, back_a, out_a), (row_b, back_b, out_b))):
        fetch.append(pltpu.make_async_copy(mine.at[pl.ds(first, rows)], own.at[k], sem_row.at[k]))
        fetch.append(pltpu.make_async_copy(theirs, back.at[k], sem_row.at[2 + k]))
        put.append(pltpu.make_async_copy(own.at[k], out.at[pl.ds(first, rows)], sem_row.at[4 + k]))
    for c in fetch:
        c.start()
    stores = [pltpu.make_async_copy(a, b, sem_out.at[k]) for k, (a, b) in enumerate(
        ((gs, gs_out), (sm, nsm_out), (gw, gw_out), (wm, nwm_out), (sw, ns_out), (ww, nw_out)))]

    def scan(moment, grad, pick):
        def body(k, total):
            r = pl.multiple_of(k * STEP, STEP)
            new = None
            part = jnp.zeros((STEP, D), jnp.float32)
            for c, block in enumerate(pick):
                cs = pl.ds(c * D, D)
                add = g[block, pl.ds(r, STEP)].astype(jnp.float32)
                grad[pl.ds(r, STEP), cs] = add
                new = MOMENTUM * moment[pl.ds(r, STEP), cs] + add
                moment[pl.ds(r, STEP), cs] = new
                part = part + new * new
            return total + part
        total = lax.fori_loop(0, D // STEP, body, jnp.zeros((STEP, D), jnp.float32))
        return jnp.sum(total)

    def scale(moment, x, total, width):
        size = jnp.sqrt(jnp.full((1, D), total, jnp.float32)) + 1e-07

        def body(k, carry):
            r = pl.multiple_of(k * STEP, STEP)
            for c in range(width // D):
                cs = pl.ds(c * D, D)
                x[pl.ds(r, STEP), cs] = (moment[pl.ds(r, STEP), cs] / size).astype(jnp.bfloat16)
            return carry
        lax.fori_loop(0, D // STEP, body, 0)

    dot_t = functools.partial(lax.dot_general, dimension_numbers=(((1,), (1,)), ((), ())),
                              preferred_element_type=jnp.float32)

    def newton(many, width):
        def body(k, carry):
            for m in range(len(many)):
                x = many[m]
                gram[m] = dot_t(x[...], x[...]).astype(jnp.bfloat16)
            for m in range(len(many)):
                a = gram[m]
                square = jnp.dot(a, a, preferred_element_type=jnp.float32)
                mix[m] = (NEWTON_TWO * a.astype(jnp.float32) + NEWTON_THREE * square).astype(jnp.bfloat16)
            for m in range(len(many)):
                x = many[m]
                for c in range(width // D):
                    cs = pl.ds(c * D, D)
                    old = x[:, cs]
                    x[:, cs] = (NEWTON_ONE * old.astype(jnp.float32)
                                + jnp.dot(mix[m], old, preferred_element_type=jnp.float32)).astype(jnp.bfloat16)
            return carry
        lax.fori_loop(0, 5, body, 0)

    def finish(weight, x, width):
        def body(k, carry):
            r = pl.multiple_of(k * STEP, STEP)
            for c in range(width // D):
                cs = pl.ds(c * D, D)
                weight[pl.ds(r, STEP), cs] = weight[pl.ds(r, STEP), cs] - MATRIX_RATE * x[pl.ds(r, STEP), cs].astype(jnp.float32)
            return carry
        lax.fori_loop(0, D // STEP, body, 0)

    loads[0].wait()
    loads[1].wait()
    for m in range(2):
        total = scan(sm.at[m], gs.at[m], (m,))
        scale(sm.at[m], xs.at[m], total, D)
    stores[0].start()
    stores[1].start()
    loads[2].wait()
    loads[3].wait()
    total = scan(wm.at[0], gw.at[0], tuple(range(2, 2 + cols)))
    scale(wm.at[0], xw, total, ff)
    stores[2].start()
    stores[3].start()
    for c in fetch:
        c.wait()
    for k in range(2):
        def join(i, carry):
            r = pl.ds(pl.multiple_of(i * 16, 16), 16)
            own[k, r] = own[k, r] + back[k, r]
            return carry
        lax.fori_loop(0, rows // 16, join, 0)
        put[k].start()
    newton([xs.at[0], xs.at[1]], D)
    loads[4].wait()
    for m in range(2):
        finish(sw.at[m], xs.at[m], D)
    stores[4].start()
    newton([xw], ff)
    loads[5].wait()
    finish(ww.at[0], xw, ff)
    stores[5].start()
    for c in stores + put:
        c.wait()


def muon(g, sw, ww, sm, wm, row_a, row_b, back_a, back_b):
    any_ = pl.BlockSpec(memory_space=pl.ANY)
    shapes = [sw, ww, sw, ww, sm, wm]
    f32 = jnp.float32
    return pl.pallas_call(
        muon_kernel,
        out_shape=tuple(jax.ShapeDtypeStruct(a.shape, f32) for a in shapes)
        + tuple(jax.ShapeDtypeStruct(a.shape, a.dtype) for a in (row_a, row_b)),
        in_specs=[any_] * 9,
        out_specs=(any_,) * 8,
        input_output_aliases={5: 6, 6: 7},
        scratch_shapes=[
            pltpu.VMEM(g.shape, jnp.bfloat16),
            pltpu.VMEM(sw.shape, f32), pltpu.VMEM(ww.shape, f32),
            pltpu.VMEM(sm.shape, f32), pltpu.VMEM(wm.shape, f32),
            pltpu.VMEM(sw.shape, f32), pltpu.VMEM(ww.shape, f32),
            pltpu.VMEM((2, D, D), jnp.bfloat16), pltpu.VMEM((D, ww.shape[2]), jnp.bfloat16),
            pltpu.VMEM((2, D, D), jnp.bfloat16), pltpu.VMEM((2, D, D), jnp.bfloat16),
            pltpu.VMEM((2,) + back_a.shape, jnp.bfloat16), pltpu.VMEM((2,) + back_a.shape, jnp.bfloat16),
            pltpu.SemaphoreType.DMA((6,)), pltpu.SemaphoreType.DMA((6,)), pltpu.SemaphoreType.DMA((6,)),
        ],
        compiler_params=pltpu.CompilerParams(vmem_limit_bytes=58 * 2**20),
        name="muon_step",
    )(g, sw, ww, sm, wm, row_a, row_b, back_a, back_b)


def shards(
    tokens,
    cotangent,
    counts,
    regions,
    square_weights,
    wide_weights,
    vectors,
    bias_table,
    square_moment,
    wide_moment,
    vector_moment,
    table_moment,
):
    meta = jnp.concatenate([counts, regions[::TOKW]])
    meta = jnp.pad(meta[None], ((0, 7), (0, 128 - meta.shape[0])))
    square_low, wide_low, tok_tail, cot_tail, meta_theirs = exchange(
        square_weights, wide_weights, tokens, cotangent, meta
    )
    hot = relative_onehot_t()
    bias = jnp.dot(hot.reshape(-1, TABLE_ROWS), bias_table, precision=HIGHEST)
    bias = bias.reshape(TOKW, IR, HEADS).transpose(0, 2, 1).reshape(TOKW, HEADS * IR)
    bias = jnp.pad(bias, ((0, JR - TOKW), (0, 0)))
    out, out_tail, gtok, gtok_tail, grads, grad_vectors, pair_sum = block(
        meta, meta_theirs, tokens, cotangent, tok_tail, cot_tail, square_low, wide_low, vectors, bias
    )
    pair_sum = pair_sum[:TOKW].reshape(TOKW, HEADS, IR)
    grad_table = jnp.einsum("jir,jhi->rh", hot, pair_sum, precision=HIGHEST)
    small = jnp.concatenate([grad_vectors.reshape(-1), grad_table.reshape(-1)])
    small = jnp.pad(small, (0, 2 * SMALL * 128 - small.shape[0])).reshape(2, SMALL, 128)
    summed, small_sum, out_back, gtok_back = make_comm(chip_grid(lax.axis_size("dp")))(
        grads, small, out_tail, gtok_tail
    )
    small_sum = small_sum.reshape(-1)
    vec_size = grad_vectors.size
    summed_vectors = small_sum[:vec_size].reshape(grad_vectors.shape)
    summed_table = small_sum[vec_size : vec_size + grad_table.size].reshape(grad_table.shape)
    owned_square, owned_wide, new_square, new_wide, new_square_moment, new_wide_moment, block_out, grad_tokens = muon(
        summed, square_weights, wide_weights, square_moment, wide_moment, out, gtok, out_back, gtok_back
    )
    slots_total = WIN_DEV * lax.axis_size("dp") * lax.axis_size("group")
    slot_root = jnp.sqrt(jnp.float32(slots_total))
    new_vector_moment = MOMENTUM * vector_moment + summed_vectors
    new_vectors = vectors - VECTOR_RATE / slot_root * new_vector_moment
    new_table_moment = MOMENTUM * table_moment + summed_table
    new_table = bias_table - TABLE_RATE / slot_root * new_table_moment
    return (
        block_out,
        grad_tokens,
        owned_square,
        owned_wide,
        summed_vectors,
        summed_table,
        new_square,
        new_wide,
        new_vectors,
        new_table,
        new_square_moment,
        new_wide_moment,
        new_vector_moment,
        new_table_moment,
    )


def solution(mesh):
    in_specs = (
        P(("dp", "group"), None),
        P(("dp", "group"), None),
        P(("dp", "group")),
        P(("dp", "group")),
        P("group", None, None),
        P("group", None, None),
        P(),
        P(),
        P("group", None, None),
        P("group", None, None),
        P(),
        P(),
    )
    out_specs = (
        P(("dp", "group"), None),
        P(("dp", "group"), None),
        P("group", None, None),
        P("group", None, None),
        P(),
        P(),
        P("group", None, None),
        P("group", None, None),
        P(),
        P(),
        P("group", None, None),
        P("group", None, None),
        P(),
        P(),
    )
    return jax.shard_map(shards, mesh=mesh, in_specs=in_specs, out_specs=out_specs, check_vma=False)
```

profile of v0, /device:TPU:0, one launch (start us, length us, event | category | flops | bytes accessed | tf_op | source)
XLA Modules:
  0.0 209.4 jit_solution(6266424083305530522)
XLA Ops:
  0.6 0.0 copy-start.1
  0.7 0.1 subtract_add_fusion
  0.8 3.0 %fusion.10 = f32[49,16,64]{2,1,0:T(8,128)S(1)} fusion(s32[49,64]{1,0:T(8,128)S(1)} %subtract_add_fusion, pred[64]{0:T(512)(128)(4,1)S(1)} %iota_compare_fusion.2, f32[169,16]{0,1:T(8,128)} %param.19), kind=kOutput, calls=%fused_computation.9 | convolution fusion | flops 102816896 | bytes 224128 | tf_op jit(solution)/shard_map/dot_general | solution.py:1003
  3.8 0.2 reshape.207
  3.9 0.7 pad.13.bias
  5.3 0.8 slice.18
  6.1 0.1 add_bitcast_fusion
  6.2 0.0 copy-done.1
  6.2 0.0 copy-start
  6.2 2.2 %copy-done = f32[1,512,2048]{2,1,0:T(8,128)S(1)} copy-done((f32[1,512,2048]{2,1,0:T(8,128)S(1)}, f32[1,512,2048]{2,1,0:T(8,128)}, u32[]{:S(2)}) %copy-start) | copy-done | bytes 4194328
  8.3 0.0 copy-start.3
  8.3 1.1 copy-done.3
  9.5 0.0 copy-start.4
  9.5 1.1 copy-done.4
  10.6 0.0 copy-start.8
  10.6 7.3 %exchange_weights.1 = (bf16[2,2,512,512]{3,2,1,0:T(8,128)(2,1)S(1)}, bf16[2,512,2048]{2,1,0:T(8,128)(2,1)S(1)}, bf16[304,512]{1,0:T(8,128)(2,1)S(1)}, bf16[304,512]{1,0:T(8,128)(2,1)S(1)}, s32[8,128]{1,0:T(8,128)S(1)}) custom-call(f32[2,512,512]{2,1,0:T(8,128)S(1)} %copy-done.1, f32[1,512,2048]{2,1,0:T(8,128)S(1)} %copy-done, ...), custom_call_target="tpu_custom_call" | custom-call | tf_op jit(solution)/shard_map/exchange_weights/pallas_call | solution.py:93
  17.9 0.0 copy-done.8
  18.0 0.0 copy-start.2
  18.0 2.0 copy-done.2
  20.0 0.0 copy-start.5
  20.0 1.3 copy-done.5
  21.3 0.0 copy-start.6
  21.3 0.7 copy-done.6
  22.0 0.0 copy-start.7
  22.0 0.7 copy-done.7
  22.7 0.0 copy-start.9
  22.7 0.6 copy-done.9
  23.3 55.4 %window_block.1 = (bf16[784,512]{1,0:T(8,128)(2,1)}, bf16[304,512]{1,0:T(8,128)(2,1)}, bf16[784,512]{1,0:T(8,128)(2,1)}, bf16[304,512]{1,0:T(8,128)(2,1)}, bf16[...) custom-call(s32[8,128]{1,0:T(8,128)} %copy-done.8, s32[8,128]{1,0:T(8,128)} %copy-done.9, ...), custom_call_target="tpu_custom_call" | custom-call | tf_op jit(solution)/shard_map/window_block/pallas_call | solution.py:373
  78.7 0.0 copy-start.12
  78.7 1.1 reshape.209
  79.8 3.7 %fusion.13 = f32[169,16]{1,0:T(8,128)S(1)} fusion(f32[49,16,64]{2,1,0:T(8,128)S(1)} %reshape.209, s32[49,64]{1,0:T(8,128)S(1)} %subtract_add_fusion, pred[64]{0:T(512)(128)(4,1)S(1)} %iota_compare_fusion.2), kind=kOutput, calls=%fused_computation.10 | convolution fusion | flops 103346880 | bytes 224128 | tf_op jit(solution)/shard_map/jir,jhi->rh/dot_general | solution.py:1010
  83.4 0.1 reshape.210
  83.5 0.0 copy-done.12
  83.6 0.6 select_maximum_fusion
  84.2 85.5 %reduce_gradients.1 = (bf16[6,512,512]{2,1,0:T(8,128)(2,1)}, f32[2,40,128]{2,1,0:T(8,128)}, bf16[304,512]{1,0:T(8,128)(2,1)}, bf16[304,512]{1,0:T(8,128)(2,1)}) custom-call(bf16[2,6,512,512]{3,2,1,0:T(8,128)(2,1)} %get-tuple-element.43.grads_ref, f32[2,40,128]{2,1,0:T(8,128)} %bitcast.15, bf16[304,512]{1,0:T(8,128)(2,1)} %get-tuple-element.46.tail_a, ...), custom_call_target="tpu_custom_call" | custom-call | tf_op jit(solution)/shard_map/reduce_gradients/pallas_call | solution.py:792
  169.7 0.0 copy-start.10
  169.7 0.0 copy-start.14
  169.8 0.0 copy-start.15
  169.8 0.0 copy-start.11
  169.8 0.0 copy-start.13
  169.8 36.5 %muon_step.1 = (f32[2,512,512]{2,1,0:T(8,128)}, f32[1,512,2048]{2,1,0:T(8,128)}, f32[2,512,512]{2,1,0:T(8,128)}, f32[1,512,2048]{2,1,0:T(8,128)}, f32[2,512,512]...) custom-call(bf16[6,512,512]{2,1,0:T(8,128)(2,1)} %get-tuple-element., ...), custom_call_target="tpu_custom_call", output_to_operand_aliasing={{6}: (5, {}), {7}: (6, {})} | custom-call | tf_op jit(solution)/shard_map/muon_step/pallas_call | solution.py:961
  206.3 0.0 copy-done.10
  206.3 0.1 slice.22
  206.4 0.0 copy-done.14
  206.5 0.1 copy.30
  206.6 0.0 copy-done.15
  206.6 0.1 copy.31
  206.7 0.7 copy.32
  207.4 0.7 copy.33
  208.1 0.7 copy.34
  208.7 0.0 copy-done.11
  208.7 0.0 copy-done.13
  208.8 0.6 multiply_subtract_fusion.1
  (7 shorter events, 0.1 us)
Async XLA Ops:
  0.6 5.5 %copy-start.1 = (f32[2,512,512]{2,1,0:T(8,128)S(1)}, f32[2,512,512]{2,1,0:T(8,128)}, u32[]{:S(2)}) copy-start(f32[2,512,512]{2,1,0:T(8,128)} %sw_hbm.1) | copy-start | bytes 6291460
  6.2 2.2 %copy-start = (f32[1,512,2048]{2,1,0:T(8,128)S(1)}, f32[1,512,2048]{2,1,0:T(8,128)}, u32[]{:S(2)}) copy-start(f32[1,512,2048]{2,1,0:T(8,128)} %ww_hbm.1) | copy-start | bytes 12582916
  8.3 1.1 copy-start.3
  9.5 1.1 copy-start.4
  10.6 7.3 %copy-start.8 = (s32[8,128]{1,0:T(8,128)}, s32[8,128]{1,0:T(8,128)S(1)}, u32[]{:S(2)}) copy-start(s32[8,128]{1,0:T(8,128)S(1)} %pad.12.meta_ref.mine) | copy-start | bytes 12292
  18.0 2.0 copy-start.2
  20.0 1.3 copy-start.5
  21.3 0.7 copy-start.6
  22.0 0.7 copy-start.7
  22.7 0.6 copy-start.9
  78.7 4.8 %copy-start.12 = (f32[12,512]{1,0:T(8,128)S(1)}, f32[12,512]{1,0:T(8,128)}, u32[]{:S(2)}) copy-start(f32[12,512]{1,0:T(8,128)} %get-tuple-element.44) | copy-start | bytes 73732
  169.7 36.6 %copy-start.10 = (f32[2,40,128]{2,1,0:T(8,128)S(1)}, f32[2,40,128]{2,1,0:T(8,128)}, u32[]{:S(2)}) copy-start(f32[2,40,128]{2,1,0:T(8,128)} %get-tuple-element.57) | copy-start | bytes 122884
  169.7 36.7 %copy-start.14 = (f32[169,16]{0,1:T(8,128)S(1)}, f32[169,16]{0,1:T(8,128)}, u32[]{:S(2)}) copy-start(f32[169,16]{0,1:T(8,128)} %param.23) | copy-start | bytes 32452
  169.8 36.8 %copy-start.15 = (f32[169,16]{0,1:T(8,128)S(1)}, f32[169,16]{0,1:T(8,128)}, u32[]{:S(2)}) copy-start(f32[169,16]{0,1:T(8,128)} %param.19) | copy-start | bytes 32452
  169.8 39.0 %copy-start.11 = (f32[12,512]{1,0:T(8,128)S(1)}, f32[12,512]{1,0:T(8,128)}, u32[]{:S(2)}) copy-start(f32[12,512]{1,0:T(8,128)} %vec.1) | copy-start | bytes 73732
  169.8 39.0 %copy-start.13 = (f32[12,512]{1,0:T(8,128)S(1)}, f32[12,512]{1,0:T(8,128)}, u32[]{:S(2)}) copy-start(f32[12,512]{1,0:T(8,128)} %param.22) | copy-start | bytes 73732
where the time goes:
time: 210 us; the launch traced here: 209 us
  Pallas kernels  185 us (88%)
  local copies, waits for them, and re-layouts  15 us (7%)
  matrix products  6.65 us (3%)
    pallas_call x1, Pallas kernels, call(): pl.pallas_call(functools.partial(kernel, delta=delta), out_shape=(jax.Sha...  85.5 us
    pallas_call x1, Pallas kernels, block(): pl.pallas_call(block_kernel, out_shape=(jax.ShapeDtypeStruct(tok.shape, b...  55.4 us
    pallas_call x1, Pallas kernels, muon(): pl.pallas_call(muon_kernel, out_shape=tuple((jax.ShapeDtypeStruct(a.shape...  36.5 us
    unnamed x37, local copies, waits for them, and re-layouts  12.1 us
    pallas_call x1, Pallas kernels, exchange(): pl.pallas_call(exchange_kernel, out_shape=(jax.ShapeDtypeStruct((2, 2, D,...  7.31 us

commit v1 on v0

--- a/solution.py
+++ b/solution.py
@@ -3,14 +3,13 @@
 
 import jax
 import jax.numpy as jnp
+import numpy as np
 from jax import lax
 from jax.experimental import pallas as pl
 from jax.experimental.pallas import tpu as pltpu
 from jax.sharding import PartitionSpec as P
 
 HIGHEST = lax.Precision.HIGHEST
-VECTOR_RATE = 0.05
-TABLE_RATE = 1.0
 D = 512
 HEADS = 16
 HEAD_DIM = 32
@@ -27,6 +26,7 @@
 PADR = 528
 TAIL0 = 480
 TAIL = WIN_DEV * TOKW - TAIL0
+SMALL = 40
 JR = 56
 IR = 64
 GH = 8
@@ -36,12 +36,21 @@
 f32, bf16 = jnp.float32, jnp.bfloat16
 
 
-def exchange_kernel(sq_hbm, wide_hbm, tok_ref, cot_ref, meta_ref,
-                    sq_out, wide_out, tok_out, cot_out, meta_out,
-                    sq_in, wide_in, tok_land, sem_in, send, recv):
+def nn(a, b):
+    return jnp.dot(a, b, preferred_element_type=f32)
+
+
+def pair_codes(shape, query_axis, entry_axis):
+    i = lax.broadcasted_iota(jnp.int32, shape, query_axis)
+    r = lax.broadcasted_iota(jnp.int32, shape, entry_axis)
+    return jnp.where(i < TOKW, i + 6 * ((i * 37) >> 8) - r, -1000), i
+
+
+def exchange_kernel(sq_hbm, wide_hbm, tok_hbm, cot_hbm, counts, regions, table,
+                    sq_out, wide_out, tok_out, cot_out, counts_out, regions_out, bias,
+                    sq_in, wide_in, sq_low, wide_low, parts, heads_first, sem_in, sem_out, send, recv):
     dp, group = lax.axis_index("dp"), lax.axis_index("group")
     partner = (dp, 1 - group)
-    ff = wide_hbm.shape[2]
     loads = [pltpu.make_async_copy(sq_hbm.at[m], sq_in.at[m], sem_in.at[m]) for m in range(2)]
     loads += [pltpu.make_async_copy(wide_hbm.at[0, pl.ds(128 * c, 128)], wide_in.at[pl.ds(128 * c, 128)], sem_in.at[2 + c])
               for c in range(4)]
@@ -55,9 +64,9 @@
         return pltpu.make_async_remote_copy(src_ref=src, dst_ref=dst, send_sem=send.at[k], recv_sem=recv.at[k],
                                             device_id=partner, device_id_type=MESH)
 
-    copies = [remote(meta_ref, meta_out, 6),
-              remote(tok_ref.at[pl.ds(TAIL0, TAIL)], tok_out, 7),
-              remote(cot_ref.at[pl.ds(TAIL0, TAIL)], cot_out, 8)]
+    copies = [remote(counts, counts_out, 6), remote(regions, regions_out, 9),
+              remote(tok_hbm.at[pl.ds(TAIL0, TAIL)], tok_out, 7),
+              remote(cot_hbm.at[pl.ds(TAIL0, TAIL)], cot_out, 8)]
     for c in copies:
         c.start()
     for m in range(2):
@@ -65,29 +74,51 @@
 
         def body(k, carry):
             r = pl.multiple_of(k * 32, 32)
-            sq_out[group, m, pl.ds(r, 32)] = sq_in[m, pl.ds(r, 32)].astype(bf16)
+            sq_low[m, pl.ds(r, 32)] = sq_in[m, pl.ds(r, 32)].astype(bf16)
             return carry
         lax.fori_loop(0, D // 32, body, 0)
-        c = remote(sq_out.at[group, m], sq_out.at[group, m], m)
-        c.start()
-        copies.append(c)
+        copies.append(remote(sq_low.at[m], sq_out.at[group, m], m))
+        copies[-1].start()
+        copies.append(pltpu.make_async_copy(sq_low.at[m], sq_out.at[group, m], sem_out.at[m]))
+        copies[-1].start()
     for q in range(4):
         loads[2 + q].wait()
 
         def body(k, carry):
             r = pl.multiple_of(q * 128 + k * 16, 16)
-            wide_out[group, pl.ds(r, 16)] = wide_in[pl.ds(r, 16)].astype(bf16)
+            wide_low[pl.ds(r, 16)] = wide_in[pl.ds(r, 16)].astype(bf16)
             return carry
         lax.fori_loop(0, 8, body, 0)
         piece = pl.ds(128 * q, 128)
-        c = remote(wide_out.at[group, piece], wide_out.at[group, piece], 2 + q)
-        c.start()
-        copies.append(c)
+        copies.append(remote(wide_low.at[piece], wide_out.at[group, piece], 2 + q))
+        copies[-1].start()
+        copies.append(pltpu.make_async_copy(wide_low.at[piece], wide_out.at[group, piece], sem_out.at[2 + q]))
+        copies[-1].start()
+
+    heads, entries = table.shape
+    parts[...] = jnp.zeros(parts.shape, f32)
+    rest = table[...]
+    for k in range(3):
+        part = rest.astype(bf16).astype(f32)
+        parts[pl.ds(heads * k, heads), pl.ds(0, entries)] = part
+        rest = rest - part
+    heads_first[...] = jnp.zeros(heads_first.shape, f32)
+    spot, _ = pair_codes((256, IR), 1, 0)
+
+    def one_key(j, carry):
+        hot = (spot == j + 6 * ((j * 37) >> 8) - 84).astype(f32).astype(bf16)
+        row = nn(parts[...].astype(bf16), hot)
+        row = row[:heads] + row[heads : 2 * heads] + row[2 * heads :]
+        heads_first[:, pl.ds(j, 1), :] = row[:, None, :]
+        return carry
+    lax.fori_loop(0, TOKW, one_key, 0)
+    for c in range(heads // 2):
+        bias[:, pl.ds(128 * c, 128)] = jnp.concatenate([heads_first[2 * c], heads_first[2 * c + 1]], axis=1)
     for c in copies:
         c.wait()
 
 
-def exchange(sq, wide, tok, cot, meta):
+def exchange(sq, wide, tok, cot, counts, regions, table):
     vmem, any_ = pl.BlockSpec(memory_space=pltpu.VMEM), pl.BlockSpec(memory_space=pl.ANY)
     ff = wide.shape[2]
     return pl.pallas_call(
@@ -97,15 +128,20 @@
             jax.ShapeDtypeStruct((2, D, ff), bf16),
             jax.ShapeDtypeStruct((TAIL, D), bf16),
             jax.ShapeDtypeStruct((TAIL, D), bf16),
-            jax.ShapeDtypeStruct(meta.shape, jnp.int32),
+            jax.ShapeDtypeStruct(counts.shape, jnp.int32),
+            jax.ShapeDtypeStruct(regions.shape, jnp.int32),
+            jax.ShapeDtypeStruct((JR, HEADS * IR), f32),
         ),
-        in_specs=[any_, any_, vmem, vmem, vmem],
-        out_specs=(vmem,) * 5,
-        scratch_shapes=[pltpu.VMEM((2, D, D), f32), pltpu.VMEM((D, ff), f32), pltpu.VMEM((8, 128), f32),
-                        pltpu.SemaphoreType.DMA((6,)), pltpu.SemaphoreType.DMA((9,)), pltpu.SemaphoreType.DMA((9,))],
-        compiler_params=pltpu.CompilerParams(collective_id=0, has_side_effects=True, vmem_limit_bytes=32 * 2**20),
+        in_specs=[any_] * 6 + [vmem],
+        out_specs=(any_,) * 6 + (vmem,),
+        scratch_shapes=[pltpu.VMEM((2, D, D), f32), pltpu.VMEM((D, ff), f32),
+                        pltpu.VMEM((2, D, D), bf16), pltpu.VMEM((D, ff), bf16),
+                        pltpu.VMEM((3 * HEADS, 256), f32), pltpu.VMEM((HEADS, JR, IR), f32),
+                        pltpu.SemaphoreType.DMA((6,)), pltpu.SemaphoreType.DMA((6,)),
+                        pltpu.SemaphoreType.DMA((10,)), pltpu.SemaphoreType.DMA((10,))],
+        compiler_params=pltpu.CompilerParams(collective_id=0, has_side_effects=True, vmem_limit_bytes=60 * 2**20),
         name="exchange_weights",
-    )(sq, wide, tok, cot, meta)
+    )(sq, wide, tok, cot, counts, regions, table)
 
 
 def nt(a, b):
@@ -114,10 +150,6 @@
 
 def tn(a, b):
     return lax.dot_general(a, b, (((0,), (0,)), ((), ())), preferred_element_type=f32)
-
-
-def nn(a, b):
-    return jnp.dot(a, b, preferred_element_type=f32)
 
 
 def loop_rows(fn, total=TALL, step=64):
@@ -127,14 +159,24 @@
     lax.fori_loop(0, total // step, body, 0)
 
 
-def block_kernel(mine, theirs, tok, cot, tok_tail, cot_tail, sq, wide, vec, bias,
-                 out, out_tail, gtok, gtok_tail, grads, gvec, gtab,
-                 x, e, norm, inv, h1, hT, qkv, mask_bias, probs, o, h2, eb, act, dact, u_s, y, dh, dx, dO, wins, dwin, tail_f):
-    count = jnp.minimum(mine[0, 0], SLOTS_RUN)
-    extra = jnp.maximum(theirs[0, 0] - SLOTS_RUN, 0)
+def block_kernel(count_ref, regions, count_other, regions_other, tok_hbm, cot_hbm, tok_tail_hbm, cot_tail_hbm, sq_hbm, wide_hbm, vec, bias,
+                 out_hbm, out_tail_hbm, gtok_hbm, gtok_tail_hbm, grads_hbm, small,
+                 tok, cot, tok_tail, cot_tail, sq, wide, out, out_tail, grads, gvec, gtab, sem_in, sem_out,
+                 x, e, norm, inv, h1, hT, qkv, mask_bias, probs, o, h2, eb, act, dact, u_s, y, dh, dx, dO, wins, dwin, tail_f, heads_first):
+    count = jnp.minimum(count_ref[0], SLOTS_RUN)
+    extra = jnp.maximum(count_other[0] - SLOTS_RUN, 0)
     ff = wide.shape[2]
     chunks = ff // D
     scale = HEAD_DIM ** (-0.5)
+    loads = [pltpu.make_async_copy(a, b, sem_in.at[k]) for k, (a, b) in enumerate((
+        (tok_hbm, tok), (tok_tail_hbm, tok_tail), (sq_hbm, sq), (cot_hbm, cot), (cot_tail_hbm, cot_tail), (wide_hbm, wide)))]
+    for c in loads:
+        c.start()
+
+    def store(src, dst, k):
+        return pltpu.make_async_copy(src, dst, sem_out.at[k])
+
+    stores = []
 
     def fill(src, src_tail, dst, masked):
         def body(rows, own):
@@ -152,8 +194,9 @@
             def _():
                 dst[pl.ds((SLOTS_RUN - 1 - k) * TOKW, TOKW)] = tail_f[pl.ds(SLOTS_RUN * TOKW - TAIL0 + k * TOKW, TOKW)]
 
+    loads[0].wait()
+    loads[1].wait()
     fill(tok, tok_tail, x, False)
-    fill(cot, cot_tail, e, True)
 
     def bias_body(c, carry):
         cs = pl.ds(pl.multiple_of(c * 128, 128), 128)
@@ -186,6 +229,7 @@
 
     norm_rows(x, vec[0:1], vec[2:3], h1, 0)
 
+    loads[2].wait()
     def project(m, carry):
         shift = jnp.where(m == 0, vec[4:5], jnp.where(m == 2, vec[5:6], jnp.zeros((1, D), f32)))
         qkv[m, pl.ds(0, TALL)] = nn(h1[...], sq[m]) + shift
@@ -230,8 +274,8 @@
         return w, pl.multiple_of(w * IR, IR), pl.ds(pl.multiple_of(hg * GC, 128), GC), pl.ds(pl.multiple_of(hg * GL, 128), GL)
 
     def kind_of(w):
-        own = mine[0, 1 + w]
-        other = theirs[0, 1 + jnp.maximum(2 * SLOTS_RUN - 1 - w, SLOTS_RUN) % WIN_DEV]
+        own = regions[w * TOKW]
+        other = regions_other[jnp.clip(2 * SLOTS_RUN - 1 - w, SLOTS_RUN, WIN_DEV - 1) * TOKW]
         region = jnp.where(w >= SLOTS_RUN - extra, other, own)
         return jnp.where(region == 1, 1, jnp.where(region == 3, 2, jnp.where(region == 4, 3, 0)))
 
@@ -251,6 +295,10 @@
 
     pack_windows(dwin.at[0], o)
 
+    loads[3].wait()
+    loads[4].wait()
+    fill(cot, cot_tail, e, True)
+
     ob = h2
     loop_rows(lambda rows: ob.__setitem__(rows, o[rows].astype(bf16)))
     y[...] = x[pl.ds(0, TALL)] + (nn(ob[...], sq[3]) + vec[6:7])
@@ -280,7 +328,11 @@
         grads[0, 2 + c] = nn(hT[1], dact[...]).astype(bf16)
         gvec[pl.ds(8 + c, 1)] = jnp.sum(dact[...].astype(f32), axis=0, keepdims=True)
         return carry
+    loads[5].wait()
     lax.fori_loop(0, chunks, feed, 0)
+    for g in range(2):
+        stores.append(store(grads.at[g, pl.ds(2, chunks)], grads_hbm.at[g, pl.ds(2, chunks)], g))
+        stores[-1].start()
 
     def norm_back(grad, gain, k, add, dst):
         zero = jnp.zeros((1, D), f32)
@@ -316,6 +368,9 @@
 
     y[...] += vec[7:8]
     put(y, out, out_tail)
+    stores += [store(out, out_hbm, 2), store(out_tail, out_tail_hbm, 3)]
+    stores[-2].start()
+    stores[-1].start()
 
     loop_rows(lambda rows: eb.__setitem__(rows, dx[rows].astype(bf16)))
     gvec[6:7] = jnp.sum(eb[...].astype(f32), axis=0, keepdims=True)
@@ -363,48 +418,83 @@
         return carry
     lax.fori_loop(0, 3, input_grads, 0)
     gvec[0:1], gvec[2:3] = norm_back(dh, vec[0:1], 0, dx, y)
-    put(y, gtok, gtok_tail)
-
-
-def block(mine, theirs, tok, cot, tok_tail, cot_tail, sq, wide, vec, bias):
+    stores.append(store(grads.at[0, pl.ds(0, 2)], grads_hbm.at[0, pl.ds(0, 2)], 4))
+    stores.append(store(grads.at[1, pl.ds(0, 2)], grads_hbm.at[1, pl.ds(0, 2)], 5))
+    stores[-2].start()
+    stores[-1].start()
+    put(y, cot, cot_tail)
+    stores += [store(cot, gtok_hbm, 6), store(cot_tail, gtok_tail_hbm, 7)]
+    stores[-2].start()
+    stores[-1].start()
+
+    half = small.shape[1]
+    for r in range(vec.shape[0]):
+        for c in range(D // 128):
+            k = r * (D // 128) + c
+            small[k // half, pl.ds(k % half, 1)] = gvec[pl.ds(r, 1), pl.ds(128 * c, 128)]
+    for h in range(HEADS):
+        heads_first[h] = gtab[:, pl.ds(IR * h, IR)]
+    spot, _ = pair_codes((IR, 256), 0, 1)
+
+    def diagonal(j, total):
+        row = heads_first[:, j]
+        high = row.astype(bf16)
+        low = (row - high.astype(f32)).astype(bf16)
+        hot = (spot == j + 6 * ((j * 37) >> 8) - 84).astype(f32).astype(bf16)
+        return total + nn(high, hot) + nn(low, hot)
+    table = jnp.zeros((HEADS, 256), f32)
+    for j in range(TOKW):
+        table = diagonal(j, table)
+    first = vec.shape[0] * (D // 128)
+    for h in range(HEADS):
+        for c in range(2):
+            k = first + 2 * h + c
+            small[k // half, pl.ds(k % half, 1)] = table[h : h + 1, 128 * c : 128 * c + 128]
+    for c in stores:
+        c.wait()
+
+
+def block(count, regions, count_other, regions_other, tok, cot, tok_tail, cot_tail, sq, wide, vec, bias):
     vmem, smem = pl.BlockSpec(memory_space=pltpu.VMEM), pl.BlockSpec(memory_space=pltpu.SMEM)
+    any_ = pl.BlockSpec(memory_space=pl.ANY)
     ff = wide.shape[2]
     V = pltpu.VMEM
+    shape = jax.ShapeDtypeStruct
+    blocks = (2, 2 + ff // D, D, D)
     return pl.pallas_call(
         block_kernel,
-        out_shape=(
-            jax.ShapeDtypeStruct(tok.shape, bf16), jax.ShapeDtypeStruct((TAIL, D), bf16),
-            jax.ShapeDtypeStruct(tok.shape, bf16), jax.ShapeDtypeStruct((TAIL, D), bf16),
-            jax.ShapeDtypeStruct((2, 2 + ff // D, D, D), bf16),
-            jax.ShapeDtypeStruct(vec.shape, f32),
-            jax.ShapeDtypeStruct((JR, HEADS * IR), f32),
-        ),
-        in_specs=[smem, smem] + [vmem] * 8,
-        out_specs=(vmem,) * 7,
+        out_shape=(shape(tok.shape, bf16), shape((TAIL, D), bf16), shape(tok.shape, bf16), shape((TAIL, D), bf16),
+                   shape(blocks, bf16), shape((2, SMALL, 128), f32)),
+        in_specs=[smem] * 4 + [any_] * 6 + [vmem] * 2,
+        out_specs=(any_,) * 5 + (vmem,),
         scratch_shapes=[
+            V(tok.shape, bf16), V(cot.shape, bf16), V((TAIL, D), bf16), V((TAIL, D), bf16), V((4, D, D), bf16),
+            V(wide.shape, bf16), V(tok.shape, bf16), V((TAIL, D), bf16), V(blocks, bf16), V(vec.shape, f32),
+            V((JR, HEADS * IR), f32), pltpu.SemaphoreType.DMA((6,)), pltpu.SemaphoreType.DMA((8,)),
             V((PADR, D), f32), V((PADR, D), f32), V((2, TALL, D), f32), V((2, TALL, 128), f32),
             V((TALL, D), bf16), V((3, D, TALL), bf16), V((3, PADR, D), f32), V((4, JR, HEADS * IR), f32),
             V((2 * SLOTS_RUN, JR, GL), f32), V((PADR, D), f32), V((TALL, D), bf16), V((TALL, D), bf16),
             V((TALL, D), bf16), V((TALL, D), bf16), V((TALL, D), f32), V((TALL, D), f32), V((TALL, D), f32),
-            V((TALL, D), f32), V((PADR, D), f32), V((4, SLOTS_RUN * IR, D), bf16), V((3, SLOTS_RUN * IR, D), f32), V((TAIL + 16, D), f32),
+            V((TALL, D), f32), V((PADR, D), f32), V((4, SLOTS_RUN * IR, D), bf16), V((3, SLOTS_RUN * IR, D), f32),
+            V((TAIL + 16, D), f32), V((HEADS, JR, IR), f32),
         ],
-        compiler_params=pltpu.CompilerParams(vmem_limit_bytes=58 * 2**20),
+        compiler_params=pltpu.CompilerParams(vmem_limit_bytes=60 * 2**20),
         name="window_block",
-    )(mine, theirs, tok, cot, tok_tail, cot_tail, sq.reshape(4, D, D), wide, vec, bias)
-
-
-def relative_onehot_t():
-    j = jnp.arange(TOKW)[:, None]
-    i = jnp.arange(IR)[None, :]
-    rel = (i // WIN - j // WIN + WIN - 1) * (2 * WIN - 1) + i % WIN - j % WIN + WIN - 1
-    hot = (rel[:, :, None] == jnp.arange(TABLE_ROWS)) & (i < TOKW)[:, :, None]
-    return hot.astype(f32)
+    )(count, regions, count_other, regions_other, tok, cot, tok_tail, cot_tail, sq.reshape(4, D, D), wide, vec, bias)
 
 
 BLK = 512
 HALF = 6
 ORDER = (2, 3, 4, 5, 0, 1)
 SMALL = 40
+
+
+PER = 9
+
+
+def own_copy(grads_ref, acc, own_sem, group, piece):
+    block, rows = ORDER[piece // 2], pl.ds((piece % 2) * (BLK // 2), BLK // 2)
+    return pltpu.make_async_copy(grads_ref.at[group, block, rows], acc.at[block, rows], own_sem.at[piece])
 
 
 def chip_grid(dp):
@@ -445,53 +535,83 @@
 
 class Plan:
     def __init__(self, sizes, pieces):
-        nx, ny, nz = sizes
         self.orders = ((0, 2, 1), (1, 2, 0))
-        self.rs, self.ag = Ids(), Ids()
+        self.rs, self.ag, self.agr = Ids(), Ids(), Ids()
         self.rows = 0
         self.slots = {}
-        half = BLK // 2
         for piece in range(pieces):
-            color = piece % 2
-            rows = half
-            for stage, dim in enumerate(self.orders[color]):
+            rows = BLK // 2
+            for stage, dim in enumerate(self.orders[piece % 2]):
                 n = sizes[dim]
                 if stage < 2:
                     rows = rows // n
-                land = {}
-                for way in ("R", "L"):
-                    for j in range(n):
-                        if (way == "R" and j > 0) or (way == "L" and j < n - 1):
-                            land[way, j] = (self.rs.take(), self.rows)
-                            self.rows += rows
-                ag_recv = self.ag.take(n)
-                self.slots[piece, stage] = (land, ag_recv)
+                one = n == 2
+                first = self.rs.take(1 if one else 2)
+                send = self.ag.take(1 if one else 2)
+                land = self.rows
+                self.rows += rows * (1 if one else 2 * (n - 1))
+                self.slots[piece, stage] = dict(
+                    rs={"R": first, "L": first if one else first + 1},
+                    land={"R": land, "L": land if one else land + rows * (n - 1)},
+                    ag={1: send, -1: send if one else send + 1},
+                    agr=self.agr.take(n),
+                )
 
 
 def make_comm(sizes):
+    if sizes == (2, 2, 4):
+        return make_pairs(sizes)
     pieces = 2 * HALF
     plan = Plan(sizes, pieces)
 
     def tasks_for(piece, env):
-        (lane_all, own_ref, core_land, acc, out_ref, land_ref, rs_send, rs_recv, ag_sl, ag_sr, ag_recv,
-         core_send_sem, core_recv_sem, partner, ends, grads_ref) = env
-        color = piece % 2
+        (lane_all, core_land, acc, out_ref, land_ref, rs_send, rs_recv, ag_send, ag_recv,
+         core_send_sem, core_recv_sem, partner, ends, grads_ref, own_sem) = env
         block = ORDER[piece // 2]
-        base = color * (BLK // 2)
         half = BLK // 2
-        order = plan.orders[color]
-        dims = [lane_all[d] for d in order]
-        tasks = []
-
-        def add_into(dst, dst_rows, dst_cols, src_row, rows, cols_w, col0=0):
+        base = (piece % 2) * half
+        dims = [lane_all[d] for d in plan.orders[piece % 2]]
+        size = [half // dims[0].n, half // dims[0].n // dims[1].n]
+        start1 = base + dims[0].i * size[0]
+        start2 = start1 + dims[1].i * size[1]
+        cols = BLK // dims[2].n
+
+        def view(stage, j, many=1):
+            if stage < 2:
+                return pl.multiple_of((base, start1)[stage] + j * size[stage], 16), many * size[stage], 0, BLK
+            begin = j * cols if isinstance(j, int) else pl.multiple_of(j * cols, 128)
+            return pl.multiple_of(start2, 16), size[1], begin, many * cols
+
+        def landing(stage, way, j, many):
+            land = plan.slots[piece, stage]["land"][way]
+            n = dims[stage].n
+            k = 0 if n == 2 else (j - 1 if way == "R" else j)
+            if stage < 2:
+                return land + k * size[stage], many * size[stage], 0, BLK
+            return land + k * size[1], size[1], 0, many * cols
+
+        def rs_copy(stage, way, j, many):
+            slot = plan.slots[piece, stage]
+            r, rows, c, width = view(stage, j, many)
+            lr, lrows, lc, lwidth = landing(stage, way, j, many)
+            return pltpu.make_async_remote_copy(
+                src_ref=acc.at[block, pl.ds(r, rows), pl.ds(c, width)],
+                dst_ref=land_ref.at[pl.ds(lr, lrows), pl.ds(lc, lwidth)],
+                send_sem=rs_send.at[slot["rs"][way]],
+                recv_sem=rs_recv.at[slot["rs"][way]],
+                device_id=dims[stage].peer(1 if way == "R" else -1),
+                device_id_type=MESH,
+            )
+
+        def add_landed(stage, way, j, many):
+            r, rows, c, width = view(stage, j, many)
+            lr, lrows, _, lwidth = landing(stage, way, j, many)
             step = min(rows, 32)
 
             def body(k, carry):
-                r = pl.multiple_of(dst_rows + k * step, 16)
-                s = pl.multiple_of(src_row + k * step, 16)
-                here = acc[block, pl.ds(r, step), dst_cols].astype(jnp.float32)
-                there = land_ref[pl.ds(s, step), pl.ds(0, cols_w)].astype(jnp.float32)
-                dst[block, pl.ds(r, step), dst_cols] = (here + there).astype(jnp.bfloat16)
+                here = pl.ds(pl.multiple_of(r + k * step, 16), step)
+                there = pl.ds(pl.multiple_of(lr + k * step, 16), step)
+                acc[block, here, pl.ds(c, width)] += land_ref[there, pl.ds(0, lwidth)]
                 return carry
 
             if rows == step:
@@ -499,86 +619,62 @@
             else:
                 lax.fori_loop(0, rows // step, body, 0)
 
-        all_cols = pl.ds(0, BLK)
-
-        r_sizes = [half // dims[0].n, half // dims[0].n // dims[1].n]
-        off0 = base
-        off1 = off0 + dims[0].i * r_sizes[0]
-        off2 = off1 + dims[1].i * r_sizes[1]
-        cols = BLK // dims[2].n
-
-        def view(stage, j):
-            if stage == 0:
-                return pl.multiple_of(off0 + j * r_sizes[0], 16), r_sizes[0], pl.ds(0, BLK), BLK
-            if stage == 1:
-                return pl.multiple_of(off1 + j * r_sizes[1], 16), r_sizes[1], pl.ds(0, BLK), BLK
-            start = j * cols if isinstance(j, int) else pl.multiple_of(j * cols, 128)
-            return pl.multiple_of(off2, 16), r_sizes[1], pl.ds(start, cols), cols
-
-        def rs_copy(stage, way, j):
-            land, _ = plan.slots[piece, stage]
-            sem, row = land[way, j]
-            lane = dims[stage]
-            r, rows, cs, width = view(stage, j)
-            return pltpu.make_async_remote_copy(
-                src_ref=acc.at[block, pl.ds(r, rows), cs],
-                dst_ref=land_ref.at[pl.ds(row, rows), pl.ds(0, width)],
-                send_sem=rs_send.at[sem],
-                recv_sem=rs_recv.at[sem],
-                device_id=lane.peer(1 if way == "R" else -1),
-                device_id_type=MESH,
-            )
+        def parts(stage, first, many):
+            if many == 0:
+                return []
+            if stage < 2:
+                return [(first, many)]
+            return [(first, many)]
 
         def rs_tick(stage, h):
             lane = dims[stage]
             n = lane.n
-            land, _ = plan.slots[piece, stage]
-            last = stage == 2
 
             @pl.when(lane.i == h)
             def _():
-                for j in range(n - 1, h - 1, -1):
+                if h > 0:
+                    rs_copy(stage, "R", h, n - h).wait_recv()
+                if h < n - 1:
                     if h > 0:
-                        rs_copy(stage, "R", j).wait_recv()
-                        r, rows, cs, width = view(stage, j)
-                        add_into(acc, r, cs, land["R", j][1], rows, width)
-                    if j > h:
-                        rs_copy(stage, "R", j).start()
-
-            @pl.when(lane.i == n - 1 - h)
+                        add_landed(stage, "R", h + 1, n - 1 - h)
+                    rs_copy(stage, "R", h + 1, n - 1 - h).start()
+                if h > 0:
+                    add_landed(stage, "R", h, 1)
+
+            g = n - 1 - h
+
+            @pl.when(lane.i == g)
             def _():
-                for j in range(0, n - h):
+                if h > 0:
+                    rs_copy(stage, "L", 0, g + 1).wait_recv()
+                if g > 0:
                     if h > 0:
-                        rs_copy(stage, "L", j).wait_recv()
-                        r, rows, cs, width = view(stage, j)
-                        add_into(acc, r, cs, land["L", j][1], rows, width)
-                    if j < n - 1 - h:
-                        rs_copy(stage, "L", j).start()
+                        add_landed(stage, "L", 0, g)
+                    rs_copy(stage, "L", 0, g).start()
+                if h > 0:
+                    add_landed(stage, "L", g, 1)
 
         def rs_end(stage):
             lane = dims[stage]
             n = lane.n
-            for j in range(n):
-                if j > 0:
-                    @pl.when(lane.i < j)
-                    def _():
-                        rs_copy(stage, "R", j).wait_send()
-                if j < n - 1:
-                    @pl.when(lane.i > j)
-                    def _():
-                        rs_copy(stage, "L", j).wait_send()
+            for h in range(n):
+                @pl.when(lane.i == h)
+                def _():
+                    if h < n - 1:
+                        rs_copy(stage, "R", h + 1, n - 1 - h).wait_send()
+                    if h > 0:
+                        rs_copy(stage, "L", 0, h).wait_send()
 
         def ag_copy(stage, j, way):
-            _, first = plan.slots[piece, stage]
-            lane = dims[stage]
-            r, rows, cs, width = view(stage, j)
-            piece_ref = out_ref.at[block, pl.ds(r, rows), cs]
+            slot = plan.slots[piece, stage]
+            r, rows, c, width = view(stage, j)
+            piece_ref = out_ref.at[block, pl.ds(r, rows), pl.ds(c, width)]
             return pltpu.make_async_remote_copy(
                 src_ref=piece_ref,
                 dst_ref=piece_ref,
-                send_sem=(ag_sr if way > 0 else ag_sl).at[first + j],
-                recv_sem=ag_recv.at[first + j],
-                device_id=lane.peer(way),
+                send_sem=ag_send.at[slot["ag"][way]],
+                recv_sem=ag_recv.at[slot["agr"] + j],
+                device_id=dims[stage].peer(way),
                 device_id_type=MESH,
             )
 
@@ -599,29 +695,33 @@
             def _():
                 ag_copy(stage, i - h, -1).wait_recv()
 
-                @pl.when(i < n - 1)
-                def _():
-                    ag_copy(stage, i - h, 1).start()
+                if n > 2:
+                    @pl.when(i < n - 1)
+                    def _():
+                        ag_copy(stage, i - h + 1, 1).wait_send()
+                        ag_copy(stage, i - h, 1).start()
 
             @pl.when(i + h <= n - 1)
             def _():
                 ag_copy(stage, i + h, 1).wait_recv()
 
-                @pl.when(i > 0)
-                def _():
-                    ag_copy(stage, i + h, -1).start()
+                if n > 2:
+                    @pl.when(i > 0)
+                    def _():
+                        ag_copy(stage, i + h - 1, -1).wait_send()
+                        ag_copy(stage, i + h, -1).start()
 
         def ag_end(stage):
             lane = dims[stage]
             n, i = lane.n, lane.i
-            for h in range(n):
-                @pl.when((i >= h) & (i < n - 1))
-                def _():
-                    ag_copy(stage, i - h, 1).wait_send()
-
-                @pl.when((i + h <= n - 1) & (i > 0))
-                def _():
-                    ag_copy(stage, i + h, -1).wait_send()
+
+            @pl.when(i < n - 1)
+            def _():
+                ag_copy(stage, 0 if n > 2 else i, 1).wait_send()
+
+            @pl.when(i > 0)
+            def _():
+                ag_copy(stage, n - 1 if n > 2 else i, -1).wait_send()
 
         def core_copy():
             return pltpu.make_async_remote_copy(
@@ -634,36 +734,28 @@
             )
 
         def first():
+            own_copy(grads_ref, acc, own_sem, partner[2], piece).wait()
             core_copy().wait_recv()
 
             def body(k, carry):
-                r = pl.multiple_of(base + k * 32, 16)
-                here = grads_ref[partner[2], block, pl.ds(r, 32)].astype(jnp.float32)
-                there = core_land[block, pl.ds(r, 32)].astype(jnp.float32)
-                acc[block, pl.ds(r, 32)] = (here + there).astype(jnp.bfloat16)
+                r = pl.ds(pl.multiple_of(base + k * 32, 16), 32)
+                acc[block, r] += core_land[block, r]
                 return carry
 
             lax.fori_loop(0, half // 32, body, 0)
 
         def copy_out():
-            r, rows, cs, width = view(2, dims[2].i)
-            out_ref[block, pl.ds(r, rows), cs] = acc[block, pl.ds(r, rows), cs]
-
-        flat = [first]
-        groups = []
+            r, rows, c, width = view(2, dims[2].i)
+            out_ref[block, pl.ds(r, rows), pl.ds(c, width)] = acc[block, pl.ds(r, rows), pl.ds(c, width)]
+
+        ticks = [[first]]
         for stage in range(3):
-            for h in range(dims[stage].n):
-                groups.append((h == 0, functools.partial(rs_tick, stage, h)))
-        groups.append((False, copy_out))
+            ticks[-1].append(functools.partial(rs_tick, stage, 0))
+            ticks.extend([functools.partial(rs_tick, stage, h)] for h in range(1, dims[stage].n))
+        ticks[-1].append(copy_out)
         for stage in (2, 1, 0):
-            for h in range(dims[stage].n):
-                groups.append((h == 0, functools.partial(ag_tick, stage, h)))
-        ticks = [[first]]
-        for joined, task in groups:
-            if joined or task is copy_out:
-                ticks[-1].append(task)
-            else:
-                ticks.append([task])
+            ticks[-1].append(functools.partial(ag_tick, stage, 0))
+            ticks.extend([functools.partial(ag_tick, stage, h)] for h in range(1, dims[stage].n))
         for stage in range(3):
             ends.append(functools.partial(rs_end, stage))
             ends.append(functools.partial(ag_end, stage))
@@ -671,11 +763,13 @@
         return core_copy, ticks
 
     def kernel(grads_ref, small_ref, tail_a, tail_b, out_ref, small_out, back_a, back_b, core_land, acc, land_ref, small_core, small_land,
-               rs_send, rs_recv, ag_sl, ag_sr, ag_recv, core_s, core_r, sm_cs, sm_cr, sm_s, sm_r, bk_s, bk_r, *, delta):
+               rs_send, rs_recv, ag_send, ag_recv, core_s, core_r, sm_cs, sm_cr, sm_s, sm_r, bk_s, bk_r, own_sem, *, delta):
         lane_all = lanes(sizes)
         dp, group = lax.axis_index("dp"), lax.axis_index("group")
         partner = (dp, 1 - group, group)
 
+        for p in range(pieces):
+            own_copy(grads_ref, acc, own_sem, group, p).start()
         barrier = pltpu.get_barrier_semaphore()
         total = 1
         pl.semaphore_signal(barrier, inc=1, device_id=partner[:2], device_id_type=MESH)
@@ -687,8 +781,8 @@
         pl.semaphore_wait(barrier, total)
 
         ends = []
-        env = (lane_all, None, core_land, acc, out_ref, land_ref, rs_send, rs_recv, ag_sl, ag_sr, ag_recv,
-               core_s, core_r, partner, ends, grads_ref)
+        env = (lane_all, core_land, acc, out_ref, land_ref, rs_send, rs_recv, ag_send, ag_recv,
+               core_s, core_r, partner, ends, grads_ref, own_sem)
 
         def sm_core():
             return pltpu.make_async_remote_copy(
@@ -765,13 +859,16 @@
             core_copy().start()
         for k in range(2):
             back(k).start()
+        for _, ticks in made:
+            for task in ticks[0]:
+                task()
+        sm0()
         table = {}
-        length = max(len(t) for _, t in made)
         for p, (_, ticks) in enumerate(made):
-            for k, tick in enumerate(ticks):
+            for k, tick in enumerate(ticks[1:]):
                 table.setdefault(int(delta * (p // 2)) + k, []).append((p, tick))
-        for k, task in enumerate((sm0, sm1, sm2, sm3, sm4)):
-            table.setdefault(1 + 2 * k, []).append((-1, [task]))
+        for k, task in enumerate((sm1, sm2, sm3, sm4)):
+            table.setdefault(2 + 2 * k, []).append((pieces, [task]))
         for when in sorted(table):
             for p, tick in sorted(table[when], key=lambda e: e[0]):
                 for task in tick:
@@ -797,8 +894,8 @@
                 jax.ShapeDtypeStruct(tail_a.shape, tail_a.dtype),
                 jax.ShapeDtypeStruct(tail_b.shape, tail_b.dtype),
             ),
-            in_specs=[vmem, vmem, vmem, vmem],
-            out_specs=[vmem, vmem, vmem, vmem],
+            in_specs=[pl.BlockSpec(memory_space=pl.ANY), vmem, pl.BlockSpec(memory_space=pl.ANY), pl.BlockSpec(memory_space=pl.ANY)],
+            out_specs=[vmem, vmem, pl.BlockSpec(memory_space=pl.ANY), pl.BlockSpec(memory_space=pl.ANY)],
             scratch_shapes=[
                 pltpu.VMEM((HALF, BLK, BLK), jnp.bfloat16),
                 pltpu.VMEM((HALF, BLK, BLK), jnp.bfloat16),
@@ -808,8 +905,7 @@
                 dma((plan.rs.count,)),
                 dma((plan.rs.count,)),
                 dma((plan.ag.count,)),
-                dma((plan.ag.count,)),
-                dma((plan.ag.count,)),
+                dma((plan.agr.count,)),
                 dma((pieces,)),
                 dma((pieces,)),
                 dma((2,)),
@@ -818,9 +914,351 @@
                 dma((sum(sizes),)),
                 dma((2,)),
                 dma((2,)),
+                dma((pieces,)),
             ],
             compiler_params=pltpu.CompilerParams(
-                collective_id=1, has_side_effects=True, vmem_limit_bytes=56 * 2**20
+                collective_id=1, has_side_effects=True, vmem_limit_bytes=60 * 2**20
+            ),
+            name="reduce_gradients",
+        )(grads, small, tail_a, tail_b)
+
+    return call
+
+
+STEPS_END = (
+    0, 8, 16, 24, 32, 40, 48, 56, 64, 72, 80, 88, 1, 9, 17, 25, 33, 41, 49, 57, 65, 2, 73, 10, 81, 18, 89, 3,
+    26, 11, 34, 19, 4, 42, 27, 12, 50, 35, 20, 58, 66, 43, 28, 51, 74, 36, 82, 59, 67, 44, 90, 75, 52, 83, 60,
+    5, 68, 91, 76, 13, 84, 21, 6, 29, 92, 14, 37, 45, 22, 30, 53, 38, 61, 46, 69, 54, 77, 62, 85, 70, 93, 78,
+    86, 94,
+)
+STEPS_INNER = (
+    0, 8, 16, 24, 32, 40, 48, 56, 64, 72, 80, 88, 1, 9, 17, 25, 2, 10, 33, 41, 18, 3, 26, 49, 57, 11, 34, 19,
+    42, 65, 73, 27, 50, 35, 58, 81, 89, 43, 66, 51, 74, 59, 82, 67, 90, 75, 83, 4, 91, 12, 20, 5, 13, 28, 21,
+    36, 44, 6, 14, 29, 52, 22, 37, 60, 45, 68, 30, 53, 76, 61, 38, 84, 69, 46, 92, 54, 77, 85, 62, 70, 93, 78,
+    86, 94,
+)
+
+
+def make_pairs(sizes):
+    pieces = 2 * HALF
+    half, quarter, eighth = BLK // 2 // 2, BLK // 2 // 4, BLK // 2
+    land_rows = half + 2 * quarter + quarter
+
+    def steps_for(piece, env):
+        (lane_all, core_land, acc, out_ref, land_ref, sends, recvs, partner, grads_ref, own_sem) = env
+        block = ORDER[piece // 2]
+        base = (piece % 2) * (BLK // 2)
+        first_lane, last_lane = (lane_all[0], lane_all[1]) if piece % 2 == 0 else (lane_all[1], lane_all[0])
+        z = lane_all[2]
+        side = lax.div(z.i, 2)
+        onward = 1 - 2 * side
+        land = piece * land_rows
+        keep = base + first_lane.i * half
+        give = base + (1 - first_lane.i) * half
+        mine_z, other_z = keep + side * quarter, keep + (1 - side) * quarter
+        c_keep, c_give = last_lane.i * eighth, (1 - last_lane.i) * eighth
+        all_cols = pl.ds(0, BLK)
+        other_x = 1 - 2 * first_lane.i
+        other_y = 1 - 2 * last_lane.i
+
+        def rows_of(start, count):
+            return pl.ds(pl.multiple_of(start, 16), count)
+
+        def cols_of(start):
+            return pl.ds(pl.multiple_of(start, 128), eighth)
+
+        def send(src, dst, k, to, leave=None):
+            leave = k if leave is None else leave
+            return pltpu.make_async_remote_copy(
+                src_ref=src, dst_ref=dst, send_sem=sends.at[piece * PER + leave], recv_sem=recvs.at[piece * PER + k],
+                device_id=to, device_id_type=MESH)
+
+        def landing(row, count):
+            return land_ref.at[pl.ds(land + row, count)]
+
+        def add(start, count, row):
+            def body(k, carry):
+                here = rows_of(start + k * 32, 32)
+                acc[block, here] += land_ref[pl.ds(pl.multiple_of(land + row + k * 32, 16), 32)]
+                return carry
+            lax.fori_loop(0, count // 32, body, 0)
+
+        def out_rows(start):
+            return out_ref.at[block, rows_of(start, quarter)]
+
+        def r1():
+            return send(acc.at[block, rows_of(give, half)], landing(0, half), 0, first_lane.peer(other_x))
+
+        def near():
+            return send(acc.at[block, rows_of(other_z, quarter)], landing(half, quarter), 1, z.peer(onward))
+
+        def near_in():
+            return send(acc.at[block, rows_of(other_z, quarter)], landing(half, quarter), 1, z.peer(-onward))
+
+        def cross():
+            return send(acc.at[block, rows_of(other_z, quarter)], landing(half + quarter, quarter), 2, z.peer(onward), 1)
+
+        def back():
+            return send(acc.at[block, rows_of(mine_z, quarter)], landing(half + quarter, quarter), 2, z.peer(-onward))
+
+        def last_half(c):
+            return land_ref.at[pl.ds(land + half + 2 * quarter, quarter), pl.ds(0, eighth)]
+
+        def r3():
+            return send(acc.at[block, rows_of(mine_z, quarter), cols_of(c_give)], last_half(0), 3, last_lane.peer(other_y))
+
+        def a3(c):
+            ref = out_ref.at[block, rows_of(mine_z, quarter), cols_of(c)]
+            return send(ref, ref, 4, last_lane.peer(other_y))
+
+        def a_near(to):
+            return send(out_rows(mine_z), out_rows(mine_z), 5, z.peer(to))
+
+        def a_cross():
+            return send(out_rows(mine_z), out_rows(mine_z), 6, z.peer(onward), 5)
+
+        def a_far_in():
+            return send(out_rows(other_z), out_rows(other_z), 6, z.peer(onward))
+
+        def a_back():
+            return send(out_rows(other_z), out_rows(other_z), 6, z.peer(-onward))
+
+        def a1(start, k):
+            return send(out_rows(start), out_rows(start), k, first_lane.peer(other_x))
+
+        x_mine, x_other = give + side * quarter, give + (1 - side) * quarter
+
+        def core_copy():
+            return pltpu.make_async_remote_copy(
+                src_ref=grads_ref.at[1 - partner[2], block, pl.ds(base, BLK // 2)],
+                dst_ref=core_land.at[block, pl.ds(base, BLK // 2)],
+                send_sem=sends.at[PER * pieces + piece], recv_sem=recvs.at[PER * pieces + piece],
+                device_id=partner[:2], device_id_type=MESH)
+
+        def begin():
+            own_copy(grads_ref, acc, own_sem, partner[2], piece).wait()
+            core_copy().wait_recv()
+
+            def body(k, carry):
+                r = pl.ds(pl.multiple_of(base + k * 32, 16), 32)
+                acc[block, r] += core_land[block, r]
+                return carry
+            lax.fori_loop(0, BLK // 2 // 32, body, 0)
+            r1().start()
+
+        def x_sum():
+            r1().wait_recv()
+            add(keep, half, 0)
+
+        def x_done():
+            a1(x_mine, 7).wait_recv()
+            a1(x_other, 8).wait_recv()
+
+        def e1():
+            x_sum()
+            near().start()
+
+        def e2():
+            cross().wait_recv()
+            add(mine_z, quarter, half + quarter)
+            r3().start()
+
+        def e3():
+            r3().wait_recv()
+            r, cs = rows_of(mine_z, quarter), cols_of(c_keep)
+            out_ref[block, r, cs] = acc[block, r, cs] + last_half(0)[...]
+            a3(c_keep).start()
+
+        def e4():
+            a3(c_give).wait_recv()
+            a_near(onward).start()
+            a1(mine_z, 7).start()
+
+        def e5():
+            a_far_in().wait_recv()
+            a1(other_z, 8).start()
+
+        def i2():
+            near_in().wait_recv()
+            add(other_z, quarter, half)
+            cross().start()
+
+        def i3():
+            cross().wait_recv()
+            add(mine_z, quarter, half + quarter)
+            back().start()
+
+        def i4():
+            a_near(-onward).wait_recv()
+            a_cross().start()
+            a1(mine_z, 7).start()
+
+        def i5():
+            a_far_in().wait_recv()
+            a_back().start()
+            a1(other_z, 8).start()
+
+        ends_sent = (r1, near, r3, lambda: a3(c_keep), lambda: a_near(onward), lambda: a1(mine_z, 7), lambda: a1(other_z, 8), core_copy)
+        inner_sent = (r1, cross, back, a_cross, a_back, lambda: a1(mine_z, 7), lambda: a1(other_z, 8), core_copy)
+        return (core_copy, (begin, e1, e2, e3, e4, e5, x_done), (begin, x_sum, i2, i3, i4, i5, x_done), ends_sent, inner_sent)
+
+    def kernel(grads_ref, small_ref, tail_a, tail_b, out_ref, small_out, back_a, back_b, core_land, acc, land_ref, small_core, small_land,
+               sends, recvs, sm_cs, sm_cr, sm_s, sm_r, bk_s, bk_r, own_sem):
+        lane_all = lanes(sizes)
+        dp, group = lax.axis_index("dp"), lax.axis_index("group")
+        partner = (dp, 1 - group, group)
+
+        for p in range(pieces):
+            own_copy(grads_ref, acc, own_sem, group, p).start()
+        barrier = pltpu.get_barrier_semaphore()
+        total = 1
+        pl.semaphore_signal(barrier, inc=1, device_id=partner[:2], device_id_type=MESH)
+        for lane in lane_all:
+            for k in range(1, lane.n):
+                to = lax.rem(lane.i + k, lane.n)
+                pl.semaphore_signal(barrier, inc=1, device_id=lane.peer(to - lane.i), device_id_type=MESH)
+                total += 1
+        pl.semaphore_wait(barrier, total)
+
+        env = (lane_all, core_land, acc, out_ref, land_ref, sends, recvs, partner, grads_ref, own_sem)
+
+        def sm_core():
+            return pltpu.make_async_remote_copy(
+                src_ref=small_ref.at[1 - group], dst_ref=small_core, send_sem=sm_cs.at[0], recv_sem=sm_cr.at[0],
+                device_id=partner[:2], device_id_type=MESH)
+
+        def sm_back():
+            return pltpu.make_async_remote_copy(
+                src_ref=small_out.at[group], dst_ref=small_out.at[group], send_sem=sm_cs.at[1], recv_sem=sm_cr.at[1],
+                device_id=partner[:2], device_id_type=MESH)
+
+        first_slot = [0, sizes[0], sizes[0] + sizes[1]]
+
+        def sm_copy(d, k):
+            lane = lane_all[d]
+            to = lax.rem(lane.i + k, lane.n)
+            return pltpu.make_async_remote_copy(
+                src_ref=small_land.at[first_slot[d] + lane.i],
+                dst_ref=small_land.at[first_slot[d] + lane.i],
+                send_sem=sm_s.at[first_slot[d] + k],
+                recv_sem=sm_r.at[first_slot[d] + lane.i],
+                device_id=lane.peer(to - lane.i), device_id_type=MESH)
+
+        def sm_wait(d, k):
+            lane = lane_all[d]
+            source = lax.rem(lane.i + k, lane.n)
+            pltpu.make_async_remote_copy(
+                src_ref=small_land.at[first_slot[d] + source],
+                dst_ref=small_land.at[first_slot[d] + source],
+                send_sem=sm_s.at[first_slot[d] + k],
+                recv_sem=sm_r.at[first_slot[d] + source],
+                device_id=lane.peer(source - lane.i), device_id_type=MESH).wait_recv()
+
+        def sm_start(d, value):
+            lane = lane_all[d]
+            small_land[first_slot[d] + lane.i] = value
+            for k in range(1, lane.n):
+                sm_copy(d, k).start()
+
+        def sm_finish(d):
+            lane = lane_all[d]
+            for k in range(1, lane.n):
+                sm_wait(d, k)
+            value = small_land[first_slot[d]]
+            for j in range(1, lane.n):
+                value = value + small_land[first_slot[d] + j]
+            return value
+
+        def sm0():
+            sm_core().wait_recv()
+            sm_start(0, small_ref[group] + small_core[...])
+
+        def sm1():
+            sm_start(1, sm_finish(0))
+
+        def sm2():
+            sm_start(2, sm_finish(1))
+
+        def sm3():
+            small_out[group] = sm_finish(2)
+            sm_back().start()
+
+        def sm4():
+            sm_back().wait_recv()
+
+        def back(k):
+            return pltpu.make_async_remote_copy(
+                src_ref=(tail_a, tail_b)[k], dst_ref=(back_a, back_b)[k], send_sem=bk_s.at[k], recv_sem=bk_r.at[k],
+                device_id=partner[:2], device_id_type=MESH)
+
+        sm_core().start()
+        made = [steps_for(p, env) for p in range(pieces)]
+        for steps in made:
+            steps[0]().start()
+        for k in range(2):
+            back(k).start()
+        small_steps = (sm0, sm1, sm2, sm3, sm4)
+
+        def run(order, kind):
+            every = len(order) // len(small_steps)
+            for index, code in enumerate(order):
+                made[code // 8][1 + kind][code % 8]()
+                if index % every == every - 1 and index // every < len(small_steps):
+                    small_steps[index // every]()
+            for steps in made:
+                for sent in steps[3 + kind]:
+                    sent().wait_send()
+
+        z = lane_all[2].i
+        at_end = (z == 0) | (z == 3)
+
+        @pl.when(at_end)
+        def _():
+            run(STEPS_END, 0)
+
+        @pl.when(jnp.logical_not(at_end))
+        def _():
+            run(STEPS_INNER, 1)
+
+        for k in range(2):
+            back(k).wait()
+        sm_core().wait_send()
+        sm_back().wait_send()
+        for d in range(3):
+            for k in range(1, sizes[d]):
+                sm_copy(d, k).wait_send()
+
+    def call(grads, small, tail_a, tail_b):
+        dma = pltpu.SemaphoreType.DMA
+        vmem = pl.BlockSpec(memory_space=pltpu.VMEM)
+        return pl.pallas_call(
+            kernel,
+            out_shape=(
+                jax.ShapeDtypeStruct((HALF, BLK, BLK), jnp.bfloat16),
+                jax.ShapeDtypeStruct((2, SMALL, 128), jnp.float32),
+                jax.ShapeDtypeStruct(tail_a.shape, tail_a.dtype),
+                jax.ShapeDtypeStruct(tail_b.shape, tail_b.dtype),
+            ),
+            in_specs=[pl.BlockSpec(memory_space=pl.ANY), vmem, pl.BlockSpec(memory_space=pl.ANY), pl.BlockSpec(memory_space=pl.ANY)],
+            out_specs=[vmem, vmem, pl.BlockSpec(memory_space=pl.ANY), pl.BlockSpec(memory_space=pl.ANY)],
+            scratch_shapes=[
+                pltpu.VMEM((HALF, BLK, BLK), jnp.bfloat16),
+                pltpu.VMEM((HALF, BLK, BLK), jnp.bfloat16),
+                pltpu.VMEM((pieces * land_rows, BLK), jnp.bfloat16),
+                pltpu.VMEM((SMALL, 128), jnp.float32),
+                pltpu.VMEM((sum(sizes), SMALL, 128), jnp.float32),
+                dma(((PER + 1) * pieces,)),
+                dma(((PER + 1) * pieces,)),
+                dma((2,)),
+                dma((2,)),
+                dma((sum(sizes),)),
+                dma((sum(sizes),)),
+                dma((2,)),
+                dma((2,)),
+                dma((pieces,)),
+            ],
+            compiler_params=pltpu.CompilerParams(
+                collective_id=1, has_side_effects=True, vmem_limit_bytes=60 * 2**20
             ),
             name="reduce_gradients",
         )(grads, small, tail_a, tail_b)
@@ -834,11 +1272,14 @@
 NEWTON_TWO = -4.775
 NEWTON_THREE = 2.0315
 STEP = 32
+VECTOR_RATE = 0.05
+TABLE_RATE = 1.0
 
 
 def muon_kernel(g_hbm, sw_hbm, ww_hbm, sm_hbm, wm_hbm, row_a, row_b, back_a, back_b,
-                gs_out, gw_out, ns_out, nw_out, nsm_out, nwm_out, out_a, out_b,
-                g, sw, ww, sm, wm, gs, gw, xs, xw, gram, mix, own, back, sem_in, sem_out, sem_row):
+                small, vec, tab, vec_m, tab_m,
+                gs_out, gw_out, ns_out, nw_out, nsm_out, nwm_out, out_a, out_b, gv_out, gt_out, nv_out, nt_out, nvm_out, ntm_out,
+                g, sw, ww, sm, wm, gs, gw, xs, xw, gram, mix, own, back, sem_in, sem_out, sem_row, *, slot_root):
     ff = ww.shape[2]
     cols = ff // D
 
@@ -941,6 +1382,24 @@
             return carry
         lax.fori_loop(0, rows // 16, join, 0)
         put[k].start()
+    half = small.shape[1]
+
+    def small_row(k):
+        return small[k // half, pl.ds(k % half, 1)]
+
+    lines = D // 128
+    for r in range(vec.shape[0]):
+        for c in range(lines):
+            gv_out[pl.ds(r, 1), pl.ds(128 * c, 128)] = small_row(r * lines + c)
+    nvm_out[...] = MOMENTUM * vec_m[...] + gv_out[...]
+    nv_out[...] = vec[...] - (VECTOR_RATE / slot_root) * nvm_out[...]
+    first = vec.shape[0] * lines
+    heads, entries = tab.shape
+    gt_out[:, pl.ds(0, 128)] = jnp.concatenate([small_row(first + 2 * h) for h in range(heads)], axis=0)
+    gt_out[:, pl.ds(128, entries - 128)] = jnp.concatenate(
+        [small_row(first + 2 * h + 1)[:, : entries - 128] for h in range(heads)], axis=0)
+    ntm_out[...] = MOMENTUM * tab_m[...] + gt_out[...]
+    nt_out[...] = tab[...] - (TABLE_RATE / slot_root) * ntm_out[...]
     newton([xs.at[0], xs.at[1]], D)
     loads[4].wait()
     for m in range(2):
@@ -954,16 +1413,18 @@
         c.wait()
 
 
-def muon(g, sw, ww, sm, wm, row_a, row_b, back_a, back_b):
-    any_ = pl.BlockSpec(memory_space=pl.ANY)
+def muon(g, sw, ww, sm, wm, row_a, row_b, back_a, back_b, small, vec, tab, vec_m, tab_m, slots):
+    any_, vmem = pl.BlockSpec(memory_space=pl.ANY), pl.BlockSpec(memory_space=pltpu.VMEM)
+    slot_root = float(np.sqrt(np.float32(slots)))
     shapes = [sw, ww, sw, ww, sm, wm]
     f32 = jnp.float32
     return pl.pallas_call(
-        muon_kernel,
+        functools.partial(muon_kernel, slot_root=slot_root),
         out_shape=tuple(jax.ShapeDtypeStruct(a.shape, f32) for a in shapes)
-        + tuple(jax.ShapeDtypeStruct(a.shape, a.dtype) for a in (row_a, row_b)),
-        in_specs=[any_] * 9,
-        out_specs=(any_,) * 8,
+        + tuple(jax.ShapeDtypeStruct(a.shape, a.dtype) for a in (row_a, row_b))
+        + tuple(jax.ShapeDtypeStruct(a.shape, f32) for a in (vec, tab, vec, tab, vec, tab)),
+        in_specs=[any_] * 9 + [vmem] * 5,
+        out_specs=(any_,) * 8 + (vmem,) * 6,
         input_output_aliases={5: 6, 6: 7},
         scratch_shapes=[
             pltpu.VMEM(g.shape, jnp.bfloat16),
@@ -977,7 +1438,7 @@
         ],
         compiler_params=pltpu.CompilerParams(vmem_limit_bytes=58 * 2**20),
         name="muon_step",
-    )(g, sw, ww, sm, wm, row_a, row_b, back_a, back_b)
+    )(g, sw, ww, sm, wm, row_a, row_b, back_a, back_b, small, vec, tab, vec_m, tab_m)
 
 
 def shards(
@@ -994,53 +1455,62 @@
     vector_moment,
     table_moment,
 ):
-    meta = jnp.concatenate([counts, regions[::TOKW]])
-    meta = jnp.pad(meta[None], ((0, 7), (0, 128 - meta.shape[0])))
-    square_low, wide_low, tok_tail, cot_tail, meta_theirs = exchange(
-        square_weights, wide_weights, tokens, cotangent, meta
+    table = bias_table.T
+    square_low, wide_low, tok_tail, cot_tail, count_other, regions_other, bias = exchange(
+        square_weights, wide_weights, tokens, cotangent, counts, regions, table
     )
-    hot = relative_onehot_t()
-    bias = jnp.dot(hot.reshape(-1, TABLE_ROWS), bias_table, precision=HIGHEST)
-    bias = bias.reshape(TOKW, IR, HEADS).transpose(0, 2, 1).reshape(TOKW, HEADS * IR)
-    bias = jnp.pad(bias, ((0, JR - TOKW), (0, 0)))
-    out, out_tail, gtok, gtok_tail, grads, grad_vectors, pair_sum = block(
-        meta, meta_theirs, tokens, cotangent, tok_tail, cot_tail, square_low, wide_low, vectors, bias
+    out, out_tail, gtok, gtok_tail, grads, small = block(
+        counts, regions, count_other, regions_other, tokens, cotangent, tok_tail, cot_tail, square_low, wide_low, vectors, bias
     )
-    pair_sum = pair_sum[:TOKW].reshape(TOKW, HEADS, IR)
-    grad_table = jnp.einsum("jir,jhi->rh", hot, pair_sum, precision=HIGHEST)
-    small = jnp.concatenate([grad_vectors.reshape(-1), grad_table.reshape(-1)])
-    small = jnp.pad(small, (0, 2 * SMALL * 128 - small.shape[0])).reshape(2, SMALL, 128)
-    summed, small_sum, out_back, gtok_back = make_comm(chip_grid(lax.axis_size("dp")))(
-        grads, small, out_tail, gtok_tail
+    dp_size, group_size = lax.axis_size("dp"), lax.axis_size("group")
+    summed, small_sum, out_back, gtok_back = make_comm(chip_grid(dp_size))(grads, small, out_tail, gtok_tail)
+    (
+        owned_square,
+        owned_wide,
+        new_square,
+        new_wide,
+        new_square_moment,
+        new_wide_moment,
+        block_out,
+        grad_tokens,
+        summed_vectors,
+        summed_table,
+        new_vectors,
+        new_table,
+        new_vector_moment,
+        new_table_moment,
+    ) = muon(
+        summed,
+        square_weights,
+        wide_weights,
+        square_moment,
+        wide_moment,
+        out,
+        gtok,
+        out_back,
+        gtok_back,
+        small_sum,
+        vectors,
+        table,
+        vector_moment,
+        table_moment.T,
+        WIN_DEV * dp_size * group_size,
     )
-    small_sum = small_sum.reshape(-1)
-    vec_size = grad_vectors.size
-    summed_vectors = small_sum[:vec_size].reshape(grad_vectors.shape)
-    summed_table = small_sum[vec_size : vec_size + grad_table.size].reshape(grad_table.shape)
-    owned_square, owned_wide, new_square, new_wide, new_square_moment, new_wide_moment, block_out, grad_tokens = muon(
-        summed, square_weights, wide_weights, square_moment, wide_moment, out, gtok, out_back, gtok_back
-    )
-    slots_total = WIN_DEV * lax.axis_size("dp") * lax.axis_size("group")
-    slot_root = jnp.sqrt(jnp.float32(slots_total))
-    new_vector_moment = MOMENTUM * vector_moment + summed_vectors
-    new_vectors = vectors - VECTOR_RATE / slot_root * new_vector_moment
-    new_table_moment = MOMENTUM * table_moment + summed_table
-    new_table = bias_table - TABLE_RATE / slot_root * new_table_moment
     return (
         block_out,
         grad_tokens,
         owned_square,
         owned_wide,
         summed_vectors,
-        summed_table,
+        summed_table.T,
         new_square,
         new_wide,
         new_vectors,
-        new_table,
+        new_table.T,
         new_square_moment,
         new_wide_moment,
         new_vector_moment,
-        new_table_moment,
+        new_table_moment.T,
     )
 
 

time: 210 us -> 171 us (0.81)
  Pallas kernels: 185 us -> 169 us
  local copies, waits for them, and re-layouts: 15 us -> 0 us
  matrix products: 6.65 us -> 0 us
    pallas_call x3, Pallas kernels: 177 us -> 156 us  [the longest x1 68.9 us: call(): pl.pallas_call(kernel, out_shape=(jax.ShapeDtypeStruct((HALF, BLK, BLK),...]
    unnamed x37 -> x0, local copies, waits for them, and re-layouts: 12.1 us -> none
    dot_general x2 -> x0, matrix products: 6.65 us -> none  [the longest x1 3.66 us: shards(): grad_table = jnp.einsum('jir,jhi->rh', hot, pair_sum, precision=HIGHEST)]
    pallas_call x1, Pallas kernels: 7.31 us -> 12.9 us  [exchange(): pl.pallas_call(exchange_kernel, out_shape=(jax.ShapeDtypeStruct((2, 2, D,...]
where the time goes in v1:
time: 171 us
  Pallas kernels  169 us (99%)
    pallas_call x1, Pallas kernels, call(): pl.pallas_call(kernel, out_shape=(jax.ShapeDtypeStruct((HALF, BLK, BLK),...  68.9 us
    pallas_call x1, Pallas kernels, block(): pl.pallas_call(block_kernel, out_shape=(shape(tok.shape, bf16), shape((TA...  53.1 us
    pallas_call x1, Pallas kernels, muon(): pl.pallas_call(functools.partial(muon_kernel, slot_root=slot_root), out_s...  34.3 us
    pallas_call x1, Pallas kernels, exchange(): pl.pallas_call(exchange_kernel, out_shape=(jax.ShapeDtypeStruct((2, 2, D,...  12.9 us

profile of v1, /device:TPU:0, one launch (start us, length us, event | category | flops | bytes accessed | tf_op | source)
XLA Modules:
  0.0 170.6 jit_solution(13873655414228287031)
XLA Ops:
  1.3 12.9 %exchange_weights.1 = (bf16[2,2,512,512]{3,2,1,0:T(8,128)(2,1)}, bf16[2,512,2048]{2,1,0:T(8,128)(2,1)}, bf16[304,512]{1,0:T(8,128)(2,1)}, bf16[304,512]{1,0:T(8,...) custom-call(f32[2,512,512]{2,1,0:T(8,128)} %sw_hbm.1, f32[1,512,2048]{2,1,0:T(8,128)} %ww_hbm.1, ...), custom_call_target="tpu_custom_call" | custom-call | tf_op jit(solution)/shard_map/exchange_weights/pallas_call | solution.py:124
  14.2 53.1 %window_block.1 = (bf16[784,512]{1,0:T(8,128)(2,1)}, bf16[304,512]{1,0:T(8,128)(2,1)}, bf16[784,512]{1,0:T(8,128)(2,1)}, bf16[304,512]{1,0:T(8,128)(2,1)}, bf16[...) custom-call(s32[1]{0:T(128)S(6)} %copy.30.counts.count_ref, s32[784]{0:T(1024)} %regions.3, ...), custom_call_target="tpu_custom_call" | custom-call | tf_op jit(solution)/shard_map/window_block/pallas_call | solution.py:464
  67.3 68.9 %reduce_gradients.1 = (bf16[6,512,512]{2,1,0:T(8,128)(2,1)}, f32[2,40,128]{2,1,0:T(8,128)}, bf16[304,512]{1,0:T(8,128)(2,1)}, bf16[304,512]{1,0:T(8,128)(2,1)}) custom-call(bf16[2,6,512,512]{3,2,1,0:T(8,128)(2,1)} %get-tuple-element.52.grads_ref, f32[2,40,128]{2,1,0:T(8,128)} %get-tuple-element.53.small_ref, bf16[304,512]{1,0:T(8,128)(2,1)} %get-tuple-element.54.tail_a, ...), custom_call_target="tpu_custom_call" | custom-call | tf_op jit(solution)/shard_map/reduce_gradients/pallas_call | solution.py:1234
  136.1 34.3 %muon_step.1 = (f32[2,512,512]{2,1,0:T(8,128)}, f32[1,512,2048]{2,1,0:T(8,128)}, f32[2,512,512]{2,1,0:T(8,128)}, f32[1,512,2048]{2,1,0:T(8,128)}, f32[2,512,512]...) custom-call(bf16[6,512,512]{2,1,0:T(8,128)(2,1)} %get-tuple-element., ...), custom_call_target="tpu_custom_call", output_to_operand_aliasing={{6}: (5, {}), {7}: (6, {})} | custom-call | tf_op jit(solution)/shard_map/muon_step/pallas_call | solution.py:1421

commit v2 on v1

--- a/solution.py
+++ b/solution.py
@@ -104,14 +104,15 @@
         rest = rest - part
     heads_first[...] = jnp.zeros(heads_first.shape, f32)
     spot, _ = pair_codes((256, IR), 1, 0)
+    parts_low = parts[...].astype(bf16)
 
     def one_key(j, carry):
         hot = (spot == j + 6 * ((j * 37) >> 8) - 84).astype(f32).astype(bf16)
-        row = nn(parts[...].astype(bf16), hot)
+        row = nn(parts_low, hot)
         row = row[:heads] + row[heads : 2 * heads] + row[2 * heads :]
         heads_first[:, pl.ds(j, 1), :] = row[:, None, :]
         return carry
-    lax.fori_loop(0, TOKW, one_key, 0)
+    lax.fori_loop(0, TOKW, one_key, 0, unroll=7)
     for c in range(heads // 2):
         bias[:, pl.ds(128 * c, 128)] = jnp.concatenate([heads_first[2 * c], heads_first[2 * c + 1]], axis=1)
     for c in copies:
@@ -156,7 +157,7 @@
     def body(k, carry):
         fn(pl.ds(pl.multiple_of(k * step, step), step))
         return carry
-    lax.fori_loop(0, total // step, body, 0)
+    lax.fori_loop(0, total // step, body, 0, unroll=4)
 
 
 def block_kernel(count_ref, regions, count_other, regions_other, tok_hbm, cot_hbm, tok_tail_hbm, cot_tail_hbm, sq_hbm, wide_hbm, vec, bias,
@@ -239,20 +240,20 @@
     live_i = lax.broadcasted_iota(jnp.int32, (IR, 1), 0) < TOKW
 
     def spread_windows(src, dst):
-        for w in range(SLOTS_RUN):
-            def body(c, carry):
-                cs = pl.ds(pl.multiple_of(c * 128, 128), 128)
+        def body(c, carry):
+            cs = pl.ds(pl.multiple_of(c * 128, 128), 128)
+            for w in range(SLOTS_RUN):
                 dst[pl.ds(w * IR, IR), cs] = jnp.where(live_i, src[pl.ds(w * TOKW, IR), cs], 0.0).astype(bf16)
-                return carry
-            lax.fori_loop(0, D // 128, body, 0)
+            return carry
+        lax.fori_loop(0, D // 128, body, 0)
 
     def pack_windows(src, dst):
-        for w in range(SLOTS_RUN):
-            def body(c, carry):
-                cs = pl.ds(pl.multiple_of(c * 128, 128), 128)
+        def body(c, carry):
+            cs = pl.ds(pl.multiple_of(c * 128, 128), 128)
+            for w in range(SLOTS_RUN):
                 dst[pl.ds(w * TOKW, TOKW), cs] = src[pl.ds(w * IR, TOKW), cs]
-                return carry
-            lax.fori_loop(0, D // 128, body, 0)
+            return carry
+        lax.fori_loop(0, D // 128, body, 0)
 
     for m in range(3):
         spread_windows(qkv.at[m], wins.at[m])
@@ -291,7 +292,7 @@
         probs[t] = p
         dwin[0, pl.ds(row, IR), cs] = gather(tn(p.astype(bf16), vb))
         return carry
-    lax.fori_loop(0, 2 * SLOTS_RUN, attend, 0)
+    lax.fori_loop(0, 2 * SLOTS_RUN, attend, 0, unroll=10)
 
     pack_windows(dwin.at[0], o)
 
@@ -321,7 +322,7 @@
             density = jnp.exp(-0.5 * u * u) * 0.3989422804014327
             act[rows] = (u * cdf).astype(bf16)
             dact[rows] = (dO[rows] * (cdf + u * density)).astype(bf16)
-        loop_rows(body, TALL, 16)
+        loop_rows(body, TALL, 64)
         y[...] += nt(act[...], wide[1, :, cs])
         dh[...] += nt(dact[...], wide[0, :, cs])
         grads[1, 2 + c] = nn(hT[2], act[...]).astype(bf16)
@@ -347,7 +348,7 @@
             dst[rows] = add[rows] + r * (dn - jnp.mean(dn, axis=1, keepdims=True)
                                          - n * jnp.mean(dn * n, axis=1, keepdims=True))
             return (g_gain + jnp.sum(g * n, axis=0, keepdims=True), g_shift + jnp.sum(g, axis=0, keepdims=True))
-        return lax.fori_loop(0, TALL // 64, body, (zero, zero))
+        return lax.fori_loop(0, TALL // 64, body, (zero, zero), unroll=2)
 
     gvec[1:2], gvec[3:4] = norm_back(dh, vec[1:2], 1, e, dx)
     gvec[7:8] = jnp.sum(e[pl.ds(0, TALL)], axis=0, keepdims=True)
@@ -394,7 +395,7 @@
         dwin[1, pl.ds(row, JR), cs] = nn(dsb, qd) * scale
         dwin[0, pl.ds(row, IR), cs] = gather(tn(dsb, kb)) * scale
         return carry
-    lax.fori_loop(0, 2 * SLOTS_RUN, attend_back, 0)
+    lax.fori_loop(0, 2 * SLOTS_RUN, attend_back, 0, unroll=10)
 
     for m in range(3):
         qkv[m, pl.ds(TALL - 24, PADR - TALL + 24)] = jnp.zeros((PADR - TALL + 24, D), f32)
@@ -1272,6 +1273,7 @@
 NEWTON_TWO = -4.775
 NEWTON_THREE = 2.0315
 STEP = 32
+H = 256
 VECTOR_RATE = 0.05
 TABLE_RATE = 1.0
 
@@ -1332,17 +1334,26 @@
     dot_t = functools.partial(lax.dot_general, dimension_numbers=(((1,), (1,)), ((), ())),
                               preferred_element_type=jnp.float32)
 
-    def newton(many, width):
+    def newton(many):
         def body(k, carry):
             for m in range(len(many)):
                 x = many[m]
-                gram[m] = dot_t(x[...], x[...]).astype(jnp.bfloat16)
+                top, low = x[pl.ds(0, H)], x[pl.ds(H, H)]
+                gram[m, pl.ds(0, H), :] = dot_t(top, x[...]).astype(jnp.bfloat16)
+                gram[m, pl.ds(H, H), pl.ds(H, H)] = dot_t(low, low).astype(jnp.bfloat16)
+                gram[m, pl.ds(H, H), pl.ds(0, H)] = gram[m, pl.ds(0, H), pl.ds(H, H)].T
             for m in range(len(many)):
                 a = gram[m]
-                square = jnp.dot(a, a, preferred_element_type=jnp.float32)
-                mix[m] = (NEWTON_TWO * a.astype(jnp.float32) + NEWTON_THREE * square).astype(jnp.bfloat16)
+
+                def poly(r, c):
+                    square = jnp.dot(a[r], a[:, c], preferred_element_type=jnp.float32)
+                    return (NEWTON_TWO * a[r, c].astype(jnp.float32) + NEWTON_THREE * square).astype(jnp.bfloat16)
+                up, down = slice(0, H), slice(H, D)
+                mix[m, pl.ds(0, H), :] = poly(up, slice(0, D))
+                mix[m, pl.ds(H, H), pl.ds(H, H)] = poly(down, down)
+                mix[m, pl.ds(H, H), pl.ds(0, H)] = mix[m, pl.ds(0, H), pl.ds(H, H)].T
             for m in range(len(many)):
-                x = many[m]
+                x, width = many[m], many[m].shape[1]
                 for c in range(width // D):
                     cs = pl.ds(c * D, D)
                     old = x[:, cs]
@@ -1400,12 +1411,11 @@
         [small_row(first + 2 * h + 1)[:, : entries - 128] for h in range(heads)], axis=0)
     ntm_out[...] = MOMENTUM * tab_m[...] + gt_out[...]
     nt_out[...] = tab[...] - (TABLE_RATE / slot_root) * ntm_out[...]
-    newton([xs.at[0], xs.at[1]], D)
+    newton([xw, xs.at[0], xs.at[1]])
     loads[4].wait()
     for m in range(2):
         finish(sw.at[m], xs.at[m], D)
     stores[4].start()
-    newton([xw], ff)
     loads[5].wait()
     finish(ww.at[0], xw, ff)
     stores[5].start()
@@ -1432,7 +1442,7 @@
             pltpu.VMEM(sm.shape, f32), pltpu.VMEM(wm.shape, f32),
             pltpu.VMEM(sw.shape, f32), pltpu.VMEM(ww.shape, f32),
             pltpu.VMEM((2, D, D), jnp.bfloat16), pltpu.VMEM((D, ww.shape[2]), jnp.bfloat16),
-            pltpu.VMEM((2, D, D), jnp.bfloat16), pltpu.VMEM((2, D, D), jnp.bfloat16),
+            pltpu.VMEM((3, D, D), jnp.bfloat16), pltpu.VMEM((3, D, D), jnp.bfloat16),
             pltpu.VMEM((2,) + back_a.shape, jnp.bfloat16), pltpu.VMEM((2,) + back_a.shape, jnp.bfloat16),
             pltpu.SemaphoreType.DMA((6,)), pltpu.SemaphoreType.DMA((6,)), pltpu.SemaphoreType.DMA((6,)),
         ],

time: 171 us -> 146 us (0.85)
  Pallas kernels: 169 us -> 144 us
    pallas_call x1, Pallas kernels: 53.1 us -> 37.1 us  [block(): pl.pallas_call(block_kernel, out_shape=(shape(tok.shape, bf16), shape((TA...]
    pallas_call x1, Pallas kernels: 34.3 us -> 29.5 us  [muon(): pl.pallas_call(functools.partial(muon_kernel, slot_root=slot_root), out_s...]
    pallas_call x1, Pallas kernels: 12.9 us -> 8.81 us  [exchange(): pl.pallas_call(exchange_kernel, out_shape=(jax.ShapeDtypeStruct((2, 2, D,...]
where the time goes in v2:
time: 146 us
  Pallas kernels  144 us (99%)
  between operations  1.48 us (1%)
    pallas_call x1, Pallas kernels, call(): pl.pallas_call(kernel, out_shape=(jax.ShapeDtypeStruct((HALF, BLK, BLK),...  68.6 us
    pallas_call x1, Pallas kernels, block(): pl.pallas_call(block_kernel, out_shape=(shape(tok.shape, bf16), shape((TA...  37.1 us
    pallas_call x1, Pallas kernels, muon(): pl.pallas_call(functools.partial(muon_kernel, slot_root=slot_root), out_s...  29.5 us
    pallas_call x1, Pallas kernels, exchange(): pl.pallas_call(exchange_kernel, out_shape=(jax.ShapeDtypeStruct((2, 2, D,...  8.81 us

profile of v2, /device:TPU:0, one launch (start us, length us, event | category | flops | bytes accessed | tf_op | source)
XLA Modules:
  0.0 145.6 jit_solution(1438448347223880447)
XLA Ops:
  1.3 8.8 %exchange_weights.1 = (bf16[2,2,512,512]{3,2,1,0:T(8,128)(2,1)}, bf16[2,512,2048]{2,1,0:T(8,128)(2,1)}, bf16[304,512]{1,0:T(8,128)(2,1)}, bf16[304,512]{1,0:T(8,...) custom-call(f32[2,512,512]{2,1,0:T(8,128)} %sw_hbm.1, f32[1,512,2048]{2,1,0:T(8,128)} %ww_hbm.1, ...), custom_call_target="tpu_custom_call" | custom-call | tf_op jit(solution)/shard_map/exchange_weights/pallas_call | solution.py:125
  10.1 37.1 %window_block.1 = (bf16[784,512]{1,0:T(8,128)(2,1)}, bf16[304,512]{1,0:T(8,128)(2,1)}, bf16[784,512]{1,0:T(8,128)(2,1)}, bf16[304,512]{1,0:T(8,128)(2,1)}, bf16[...) custom-call(s32[1]{0:T(128)S(6)} %copy.30.counts.count_ref, s32[784]{0:T(1024)} %regions.3, ...), custom_call_target="tpu_custom_call" | custom-call | tf_op jit(solution)/shard_map/window_block/pallas_call | solution.py:465
  47.2 68.6 %reduce_gradients.1 = (bf16[6,512,512]{2,1,0:T(8,128)(2,1)}, f32[2,40,128]{2,1,0:T(8,128)}, bf16[304,512]{1,0:T(8,128)(2,1)}, bf16[304,512]{1,0:T(8,128)(2,1)}) custom-call(bf16[2,6,512,512]{3,2,1,0:T(8,128)(2,1)} %get-tuple-element.52.grads_ref, f32[2,40,128]{2,1,0:T(8,128)} %get-tuple-element.53.small_ref, bf16[304,512]{1,0:T(8,128)(2,1)} %get-tuple-element.54.tail_a, ...), custom_call_target="tpu_custom_call" | custom-call | tf_op jit(solution)/shard_map/reduce_gradients/pallas_call | solution.py:1235
  115.9 29.5 %muon_step.1 = (f32[2,512,512]{2,1,0:T(8,128)}, f32[1,512,2048]{2,1,0:T(8,128)}, f32[2,512,512]{2,1,0:T(8,128)}, f32[1,512,2048]{2,1,0:T(8,128)}, f32[2,512,512]...) custom-call(bf16[6,512,512]{2,1,0:T(8,128)(2,1)} %get-tuple-element., ...), custom_call_target="tpu_custom_call", output_to_operand_aliasing={{6}: (5, {}), {7}: (6, {})} | custom-call | tf_op jit(solution)/shard_map/muon_step/pallas_call | solution.py:1431
